TPU v7x, 128 devices: a whole 4x4x4 slice. The times are simulated.
128 devices in a mesh: fsdp: 16 (over z, y_hi, core), tp: 8 (over x, y_lo).
Axes of the slice: x: 4, y: 4 (y_hi: 2, y_lo: 2; y = y_hi * 2 + y_lo), z: 4, core: 2. Of those that a mesh axis runs over, the one named last changes fastest.
Arguments:
- param: bfloat16 [1, 8192, 8192], P(None, 'fsdp', 'tp'), may hold values from -0.0625 to 0.0625
- grad: bfloat16 [1, 8192, 8192], P(None, 'fsdp', 'tp'), may hold values from -1500 to 1500
- m_codes: bfloat16 [262144, 256], P(('fsdp', 'tp')), may hold values from -1 to 1
- v_codes: bfloat16 [262144, 256], P(('fsdp', 'tp')), may hold values from 0.049804688 to 1
- m_scales: bfloat16 [262144], P(('fsdp', 'tp')), may hold values from 0.0099487305 to 0.099609375
- v_scales: bfloat16 [262144], P(('fsdp', 'tp')), may hold values from 0.0009994507 to 0.099609375
- block_target: int32 [262144], P(('fsdp', 'tp')), may hold values from 0 to 262143, as said below
Outputs:
- new_param: bfloat16 [1, 8192, 8192], P(None, 'fsdp', 'tp')
- new_m_codes: bfloat16 [1, 8192, 8192], P(None, 'fsdp', 'tp')
- new_m_scales: float32 [1, 8192, 32], P(None, 'fsdp', 'tp')
- new_v_codes: bfloat16 [1, 8192, 8192], P(None, 'fsdp', 'tp')
- new_v_scales: float32 [1, 8192, 32], P(None, 'fsdp', 'tp')
Inputs may be any that keep to these rules, and one draw needn't show every extreme that they name: block_target is a permutation of 0 to 262143. Of the 2048 saved blocks of one device, exactly 16 have their target on each device of the weights' layout.
All inputs are finite; a program needn't handle non-finite values. Where the computation divides by a largest or mean magnitude, that divisor is 1e-20 or more.
Results may differ from a plain program's by a relative error of at most 0.001.
Values may be sent and summed in bfloat16 or wider, within the bound.
No kernel may reach another device: no remote copies, remote signals or barrier semaphores. Data moves between devices by JAX's collectives and lax.ppermute only.
A program may use at most 64 MiB of HBM per device.

v0:
```python
import functools

import jax
import jax.numpy as jnp
from jax import lax
from jax.sharding import Mesh
from jax.sharding import PartitionSpec as P

D = 8192
LAYERS = 1
BLOCK = 256
FSDP = ("fsdp_0", "fsdp_1", "fsdp_2")
TP = ("tp_0", "tp_1")
FSDP_TP = ("fsdp_0", "fsdp_1", "fsdp_2", "tp_0", "tp_1")


beta_one = 0.9
beta_two = 0.999
step_count = 1000.0
learn_rate = 0.002
clip_level = 0.5
guard = 1e-06
adam_eps = 1e-08


def by_axis(shard, axes):
    return functools.reduce(lax.psum, axes, shard)


def sent_together(arrays, axis, split_dim, concat_dim, along):
    ends, at = ([], 0)
    for a in arrays[:-1]:
        at += a.shape[along]
        ends.append(at)
    both = jnp.concatenate(arrays, axis=along)
    return tuple(
        jnp.split(
            lax.all_to_all(both, axis, split_axis=split_dim, concat_axis=concat_dim, tiled=True),
            ends,
            axis=along,
        )
    )


def requantize(values):
    largest = jnp.max(jnp.abs(values), axis=-1)
    quantized = (values / (largest[..., None] + guard)).astype(jnp.bfloat16)
    return (quantized, largest)


def body(param, grad, m_codes, v_codes, m_scales, v_scales, block_target):
    fsdp_ways = lax.axis_size(FSDP)
    tp_ways = lax.axis_size(TP)
    peer_count = fsdp_ways * tp_ways
    layer_count, rows_dev, cols_dev = param.shape
    width_blocks = D // BLOCK
    layer_blocks = D * width_blocks
    local_blocks = cols_dev // BLOCK
    saved_count = m_codes.shape[0]
    per_peer = saved_count // peer_count
    layer_of = block_target // layer_blocks
    within = block_target % layer_blocks
    row_of = within // width_blocks
    column_block = within % width_blocks
    destination = row_of // rows_dev * tp_ways + column_block // local_blocks
    position = (
        layer_of * rows_dev + row_of % rows_dev
    ) * local_blocks + column_block % local_blocks
    ordering = jnp.argsort(destination, stable=True)
    both_codes = jnp.take(jnp.concatenate([m_codes, v_codes], axis=1), ordering, axis=0)
    both_scales = jnp.take(jnp.stack([m_scales, v_scales], axis=1), ordering, axis=0)
    positions = jnp.take(position, ordering, axis=0)
    square_sum = by_axis(jnp.sum(jnp.square(grad.astype(jnp.float32))), FSDP_TP)
    recv_codes, recv_scales, recv_places = (
        *sent_together(
            (
                both_codes.reshape(peer_count, per_peer, 2 * BLOCK),
                both_scales.reshape(peer_count, per_peer, 2),
            ),
            FSDP_TP,
            0,
            0,
            2,
        ),
        lax.all_to_all(
            positions.reshape(peer_count, per_peer),
            FSDP_TP,
            split_axis=0,
            concat_axis=0,
            tiled=True,
        ),
    )
    recv_codes = recv_codes.reshape(saved_count, 2 * BLOCK)
    recv_scales = recv_scales.reshape(saved_count, 2)
    recv_places = recv_places.reshape(saved_count).astype(jnp.int32)
    arranged = jnp.zeros((saved_count, 2 * BLOCK), jnp.bfloat16).at[recv_places].set(recv_codes)
    arranged_scales = (
        jnp.zeros((saved_count, 2), jnp.bfloat16)
        .at[recv_places]
        .set(recv_scales)
        .astype(jnp.float32)
    )
    block_shape = (layer_count, rows_dev, local_blocks, BLOCK)
    m_prev = (arranged[:, :BLOCK].astype(jnp.float32) * arranged_scales[:, 0:1]).reshape(
        block_shape
    )
    v_prev = (arranged[:, BLOCK:].astype(jnp.float32) * arranged_scales[:, 1:2]).reshape(
        block_shape
    )
    root_mean = jnp.sqrt(square_sum / (LAYERS * D * D) + guard)
    factor = jnp.minimum(1.0, clip_level / root_mean)
    clipped = grad.astype(jnp.float32).reshape(block_shape) * factor
    m_next = beta_one * m_prev + (1.0 - beta_one) * clipped
    v_next = beta_two * v_prev + (1.0 - beta_two) * clipped * clipped
    update = (
        m_next
        / (1.0 - beta_one**step_count)
        / (jnp.sqrt(v_next / (1.0 - beta_two**step_count)) + adam_eps)
    )
    new_param = (param.astype(jnp.float32) - learn_rate * update.reshape(param.shape)).astype(
        jnp.bfloat16
    )
    m_quant, m_large = requantize(m_next)
    v_quant, v_large = requantize(v_next)
    return (new_param, m_quant.reshape(param.shape), m_large, v_quant.reshape(param.shape), v_large)


def solution(mesh):
    torus = Mesh(
        mesh.devices.reshape(4, 2, 2, 4, 2), ("fsdp_0", "fsdp_1", "fsdp_2", "tp_0", "tp_1")
    )
    placed = (
        P(None, FSDP, TP),
        P(None, FSDP, TP),
        P(FSDP_TP, None),
        P(FSDP_TP, None),
        P(FSDP_TP),
        P(FSDP_TP),
        P(FSDP_TP),
    )
    return jax.shard_map(
        body,
        mesh=torus,
        in_specs=placed,
        out_specs=(
            P(None, FSDP, TP),
            P(None, FSDP, TP),
            P(None, FSDP, TP),
            P(None, FSDP, TP),
            P(None, FSDP, TP),
        ),
        check_vma=False,
    )
```

profile of v0, /device:TPU:1, one launch (start us, length us, event | category | flops | bytes accessed | tf_op | source)
XLA Modules:
  0.0 170.1 jit_solution(12681512910625901986)
XLA Ops:
  0.6 0.7 fusion.10
  1.4 5.0 %sort.17 = (s32[2048]{0:T(1024)}, s32[2048]{0:T(1024)S(1)}) sort(s32[2048]{0:T(1024)S(1)} %get-tuple-element.38, s32[2048]{0:T(1024)S(1)} %iota.4), dimensions={0}, to_apply=%region_0.1 | sort | flops 22528 | bytes 32768 | tf_op jit(solution)/shard_map/jit(argsort)/sort | solution.py:69
  6.4 11.8 %gather_fusion = s32[2048]{0:T(1024)S(1)} fusion(s32[2048]{0:T(1024)S(1)} %get-tuple-element.39, s32[2048]{0:T(1024)S(1)} %fusion.19), kind=kCustom, calls=%fused_computation | custom fusion | bytes 24576 | tf_op jit(solution)/shard_map/jit(_take)/gather | solution.py:72
  18.2 0.7 select_n.87
  18.9 11.5 %all-to-all-start = ((s32[128,1,16]{2,1,0:T(1,128)}), s32[128,1,16]{2,1,0:T(1,128)S(1)}, u32[]{:S(2)}, u32[]{:S(2)}) async-start(s32[128,1,16]{2,1,0:T(1,128)} %bitcast), calls=%async_computation | async-start | bytes 131072 | tf_op jit(solution)/shard_map/all_to_all | solution.py:85
  30.5 0.1 broadcast_in_dim.43
  30.6 0.3 copy.32
  30.9 6.2 %gather_fusion.2 = bf16[2048,2]{1,0:T(8,128)(2,1)S(1)} fusion(bf16[2048,2]{1,0:T(8,128)(2,1)S(1)} %copy.32, s32[2048]{0:T(1024)S(1)} %fusion.19), kind=kCustom, calls=%fused_computation.2 | custom fusion | bytes 24576 | tf_op jit(solution)/shard_map/jit(_take)/gather | solution.py:71
  37.1 1.7 pad_maximum_fusion.1
  38.8 9.2 %gather_fusion.1 = bf16[2048,512]{1,0:T(8,128)(2,1)} fusion(bf16[2048,512]{1,0:T(8,128)(2,1)S(1)} %pad_maximum_fusion.1, s32[2048]{0:T(1024)S(1)} %fusion.19), kind=kCustom, calls=%fused_computation.1 | custom fusion | bytes 4202496 | tf_op jit(solution)/shard_map/jit(_take)/gather | solution.py:70
  48.0 0.3 broadcast_select_fusion.1
  48.3 1.8 %broadcast_select_fusion = bf16[128,16,512]{2,1,0:T(8,128)(2,1)S(1)} fusion(bf16[128,16,512]{2,1,0:T(8,128)(2,1)} %bitcast.8, pred[128,16]{1,0:T(8,128)(4,1)S(1)} %broadcast_in_dim.43), kind=kLoop, calls=%fused_computation.23 | loop fusion | flops 1048576 | bytes 4196352 | tf_op jit(solution)/shard_map/jit(_take)/select_n | solution.py:70
  50.1 1.8 %pad_maximum_fusion = bf16[128,16,514]{2,1,0:T(8,128)(2,1)} fusion(bf16[128,16,2]{2,1,0:T(8,128)(2,1)S(1)} %broadcast_select_fusion.1, bf16[128,16,512]{2,1,0:T(8,128)(2,1)S(1)} %broadcast_select_fusion), kind=kLoop, calls=%fused_computation.9 | loop fusion | flops 4210688 | bytes 4210688 | tf_op jit(solution)/shard_map/concatenate | solution.py:35
  51.9 0.0 all-to-all-done
  51.9 9.8 %all-to-all-start.1 = ((bf16[128,16,514]{2,1,0:T(8,128)(2,1)}), bf16[128,16,514]{2,1,0:T(8,128)(2,1)S(1)}, u32[]{:S(2)}, u32[]{:S(2)}) async-start(bf16[128,16,514]{2,1,0:T(8,128)(2,1)} %pad_maximum_fusion), calls=%async_computation.1 | async-start | bytes 5242880 | tf_op jit(solution)/shard_map/all_to_all | solution.py:38
  61.7 2.4 %fusion = f32[]{:T(128)} fusion(bf16[1,512,1024]{2,1,0:T(8,128)(2,1)} %param.8), kind=kLoop, calls=%fused_computation.10 | loop fusion | flops 1572863 | bytes 1048580 | tf_op jit(solution)/shard_map/reduce_sum | solution.py:73
  64.0 13.4 %psum.35 = f32[]{:T(128)} all-reduce(f32[]{:T(128)} %fusion), channel_id=1, replica_groups=mesh['fsdp_0'=4,'fsdp_1'=2,'fsdp_2'=2,'tp_0'=4,'tp_1'=2] {'fsdp_0'}, use_global_device_ids=true, to_apply=%region_4.5 | all-reduce | flops 1 | bytes 8 | tf_op jit(solution)/shard_map/psum | solution.py:27
  77.4 10.8 %psum.36 = f32[]{:T(128)} all-reduce(f32[]{:T(128)} %psum.35), channel_id=1, replica_groups=mesh['fsdp_0'=4,'fsdp_1'=2,'fsdp_2'=2,'tp_0'=4,'tp_1'=2] {'fsdp_1'}, use_global_device_ids=true, to_apply=%region_5.6 | all-reduce | flops 1 | bytes 8 | tf_op jit(solution)/shard_map/psum | solution.py:27
  88.2 7.9 %psum.37 = f32[]{:T(128)} all-reduce(f32[]{:T(128)} %psum.36), channel_id=1, replica_groups=mesh['fsdp_0'=4,'fsdp_1'=2,'fsdp_2'=2,'tp_0'=4,'tp_1'=2] {'fsdp_2'}, use_global_device_ids=true, to_apply=%region_6.7 | all-reduce | flops 1 | bytes 8 | tf_op jit(solution)/shard_map/psum | solution.py:27
  96.1 17.3 %psum.38 = f32[]{:T(128)} all-reduce(f32[]{:T(128)} %psum.37), channel_id=1, replica_groups=mesh['fsdp_0'=4,'fsdp_1'=2,'fsdp_2'=2,'tp_0'=4,'tp_1'=2] {'tp_0'}, use_global_device_ids=true, to_apply=%region_7.8 | all-reduce | flops 1 | bytes 8 | tf_op jit(solution)/shard_map/psum | solution.py:27
  113.4 4.4 %psum.39 = f32[]{:T(128)} all-reduce(f32[]{:T(128)} %psum.38), channel_id=1, replica_groups=mesh['fsdp_0'=4,'fsdp_1'=2,'fsdp_2'=2,'tp_0'=4,'tp_1'=2] {'tp_1'}, use_global_device_ids=true, to_apply=%region_8.9 | all-reduce | flops 1 | bytes 8 | tf_op jit(solution)/shard_map/psum | solution.py:27
  118.4 2.9 %convert_multiply_fusion = f32[1,512,1024]{2,1,0:T(8,128)} fusion(bf16[1,512,1024]{2,1,0:T(8,128)(2,1)} %param.8, f32[]{:T(128)S(6)} %min.3), kind=kLoop, calls=%fused_computation.7 | loop fusion | flops 1048576 | bytes 3145732 | tf_op jit(solution)/shard_map/mul | solution.py:112
  121.3 2.9 %mul.183 = f32[2048,256]{1,0:T(8,128)} reshape(f32[1,512,1024]{2,1,0:T(8,128)} %convert_multiply_fusion) | data formatting | bytes 4194304 | tf_op jit(solution)/shard_map/mul | solution.py:112
  124.2 0.5 broadcast.204
  124.7 0.8 reduce.9
  125.5 0.1 reshape.196
  125.6 0.0 all-to-all-done.1
  125.6 1.7 split.8
  127.3 11.5 %scatter_custom_fusion = bf16[2048,512]{1,0:T(8,128)(2,1)} fusion(s32[2048]{0:T(1024)S(1)} %bitcast.12, bf16[2048,512]{1,0:T(8,128)(2,1)} %bitcast.10, bf16[]{:T(256)} %constant.133.clone.1), kind=kCustom, calls=%fused_computation.26 | custom fusion | bytes 2097664 | tf_op jit(solution)/shard_map/scatter | solution.py:96
  138.8 0.1 split.9
  138.9 6.0 %scatter_custom_fusion.1 = bf16[2048,2]{1,0:T(8,128)(2,1)S(1)} fusion(s32[2048]{0:T(1024)S(1)} %bitcast.13, bf16[2048,2]{1,0:T(8,128)(2,1)S(1)} %bitcast.11, bf16[]{:T(256)} %constant.133.clone.1), kind=kCustom, calls=%fused_computation.29 | custom fusion | bytes 8194 | tf_op jit(solution)/shard_map/scatter | solution.py:100
  145.0 0.1 convert_element_type.33
  145.0 0.9 slice_reduce_fusion
  146.0 0.6 copy-done.3
  146.6 2.8 %fusion.4 = (f32[2048]{0:T(1024)S(1)}, f32[2048]{0:T(1024)S(1)}, f32[2048,256]{1,0:T(8,128)}, f32[2048,256]{1,0:T(8,128)}) fusion(f32[2048,256]{1,0:T(8,128)S(1)} %copy-done.1, f32[2048]{0:T(1024)S(1)} %get-tuple-element.29, bf16[2048,512]{1,0:T(8,128)(2,1)S(1)} %copy-done.3, f32[2048]{0:T(1024)S(1)} %get-tuple-element.30), kind=kLoop, calls=%fused_computation.14 | loop fusion | flops 7860224 | bytes 8421376 | tf_op jit(solution)/shard_map/reduce_max | solution.py:46
  149.3 0.3 reduce_max.23
  149.6 0.3 reduce_max.25
  149.9 2.8 %mul.167 = f32[1,512,1024]{2,1,0:T(8,128)} reshape(f32[2048,256]{1,0:T(8,128)} %get-tuple-element.36) | data formatting | bytes 4194304 | tf_op jit(solution)/shard_map/mul | solution.py:113
  152.7 0.3 add.152
  153.0 0.7 copy.35
  153.7 0.7 copy.36
  154.4 0.3 add.149
  154.7 0.6 div.110
  155.3 2.1 %div.111 = f32[1,512,1024]{2,1,0:T(8,128)} reshape(f32[512,4,256]{2,1,0:T(4,128)S(1)} %div.110) | data formatting | bytes 4194304 | tf_op jit(solution)/shard_map/div | solution.py:47
  157.3 0.6 div.113
  158.0 2.1 %div.114 = f32[1,512,1024]{2,1,0:T(8,128)} reshape(f32[512,4,256]{2,1,0:T(4,128)S(1)} %div.113) | data formatting | bytes 4194304 | tf_op jit(solution)/shard_map/div | solution.py:47
  160.1 3.0 %mul.177 = f32[1,512,1024]{2,1,0:T(8,128)} reshape(f32[2048,256]{1,0:T(8,128)} %get-tuple-element.37) | data formatting | bytes 4194304 | tf_op jit(solution)/shard_map/mul | solution.py:114
  163.1 7.0 %divide_convert_fusion = (bf16[1,512,1024]{2,1,0:T(8,128)(2,1)}, bf16[1,512,1024]{2,1,0:T(8,128)(2,1)}, bf16[1,512,1024]{2,1,0:T(8,128)(2,1)}) fusion(f32[1,512,1024]{2,1,0:T(8,128)} %div.114, f32[1,512,1024]{2,1,0:T(8,128)} %mul.177, f32[]{:T(128)S(6)} %min.3, bf16[1,512,1024]{2,1,0:T(8,128)(2,1)S(1)} %copy-done, f32[1,512,1024]{2,1,0:T(8,128)S(1)} %copy-done.2, ...), kind=kLoop, calls=%fused_computation.16 | loop fusion | flops 9437184 | bytes 13631492 | tf_op jit(solution)/shard_map/convert_element_type | solution.py:47
  (19 shorter events, 0.1 us)
Async XLA Ops:
  6.4 24.0 %copy-start.4 = (bf16[2048]{0:T(1024)(128)(2,1)S(1)}, bf16[2048]{0:T(1024)(128)(2,1)}, u32[]{:S(2)}) copy-start(bf16[2048]{0:T(1024)(128)(2,1)} %param.11) | copy-start | bytes 12292
  6.4 24.0 %copy-start.5 = (bf16[2048]{0:T(1024)(128)(2,1)S(1)}, bf16[2048]{0:T(1024)(128)(2,1)}, u32[]{:S(2)}) copy-start(bf16[2048]{0:T(1024)(128)(2,1)} %param.12) | copy-start | bytes 12292
  18.9 32.9 %all-to-all-start = ((s32[128,1,16]{2,1,0:T(1,128)}), s32[128,1,16]{2,1,0:T(1,128)S(1)}, u32[]{:S(2)}, u32[]{:S(2)}) async-start(s32[128,1,16]{2,1,0:T(1,128)} %bitcast), calls=%async_computation | async-start | bytes 131072 | tf_op jit(solution)/shard_map/all_to_all | solution.py:85
  51.9 73.7 %all-to-all-start.1 = ((bf16[128,16,514]{2,1,0:T(8,128)(2,1)}), bf16[128,16,514]{2,1,0:T(8,128)(2,1)S(1)}, u32[]{:S(2)}, u32[]{:S(2)}) async-start(bf16[128,16,514]{2,1,0:T(8,128)(2,1)} %pad_maximum_fusion), calls=%async_computation.1 | async-start | bytes 5242880 | tf_op jit(solution)/shard_map/all_to_all | solution.py:38
  138.9 7.1 %copy-start.1 = (f32[2048,256]{1,0:T(8,128)S(1)}, f32[2048,256]{1,0:T(8,128)}, u32[]{:S(2)}) copy-start(f32[2048,256]{1,0:T(8,128)} %mul.183) | copy-start | bytes 6291460
  145.0 1.6 copy-start.3
  160.1 3.0 %copy-start = (bf16[1,512,1024]{2,1,0:T(8,128)(2,1)S(1)}, bf16[1,512,1024]{2,1,0:T(8,128)(2,1)}, u32[]{:S(2)}) copy-start(bf16[1,512,1024]{2,1,0:T(8,128)(2,1)} %param.8) | copy-start | bytes 3145732
  160.1 3.0 %copy-start.2 = (f32[1,512,1024]{2,1,0:T(8,128)S(1)}, f32[1,512,1024]{2,1,0:T(8,128)}, u32[]{:S(2)}) copy-start(f32[1,512,1024]{2,1,0:T(8,128)} %mul.167) | copy-start | bytes 6291460
where the time goes:
time: 173 us; the launch traced here: 170 us
  local copies, waits for them, and re-layouts  66.2 us (38%)
  blocking collectives  53.7 us (31%)
  other arithmetic  27.3 us (16%)
  starting transfers between devices  21.2 us (12%)
    psum x5, blocking collectives, by_axis(): return functools.reduce(lax.psum, axes, shard)  53.7 us
    gather x1, local copies, waits for them, and re-layouts, body(): positions = jnp.take(position, ordering, axis=0)  11.8 us
    scatter x1, local copies, waits for them, and re-layouts, body(): jnp.zeros((saved_count, 2 * BLOCK), jnp.bfloat16).at[recv_places]  11.5 us
    all_to_all x1, starting transfers between devices, body(): lax.all_to_all(positions.reshape(peer_count, per_peer), FSDP_TP, split_ax...  11.5 us
    all_to_all x1, starting transfers between devices, sent_together(): lax.all_to_all(both, axis, split_axis=split_dim, concat_axis=concat_dim,...  9.76 us
    gather x1, local copies, waits for them, and re-layouts, body(): jnp.take(jnp.concatenate([m_codes, v_codes], axis=1), ordering, axis=0)  9.16 us
    convert_element_type x1, other arithmetic, requantize(): quantized = (values / (largest[..., None] + guard)).astype(jnp.bfloat16)  7.01 us
    gather x1, local copies, waits for them, and re-layouts, body(): jnp.take(jnp.stack([m_scales, v_scales], axis=1), ordering, axis=0)  6.19 us
  transfers between devices with their start and end apart: 2, of which 0 were waited for; matrix products, arithmetic and copies ran while one was open for 18% of the time, Pallas kernels for 0%

commit v1 on v0

v1 whole, which is shorter than its diff:
```python
import functools

import jax
import jax.numpy as jnp
from jax import lax
from jax.experimental import pallas as pl
from jax.experimental.pallas import tpu as pltpu
from jax.sharding import Mesh
from jax.sharding import PartitionSpec as P

D = 8192
LAYERS = 1
BLOCK = 256
FSDP = ("fsdp_0", "fsdp_1", "fsdp_2")
TP = ("tp_0", "tp_1")
FSDP_TP = ("fsdp_0", "fsdp_1", "fsdp_2", "tp_0", "tp_1")

PEERS = 128
PAIR = 16
SAVED = 2048
ROWS = 512
COLB = 4
N_TP = 8
LANES = 128
CHUNKS = SAVED // LANES
HALVES = BLOCK // LANES
MSG_ROWS = PAIR * HALVES
SIDE = 8

beta_one = 0.9
beta_two = 0.999
step_count = 1000.0
learn_rate = 0.002
clip_level = 0.5
guard = 1e-06
adam_eps = 1e-08

F32 = jnp.float32
BF16 = jnp.bfloat16
INTERPRET = False


def iota(shape, dim):
    return lax.broadcasted_iota(jnp.int32, shape, dim)


def one_hot(condition):
    return jnp.where(condition, 1.0, 0.0).astype(BF16)


def times(a, b):
    return jnp.dot(a, b, preferred_element_type=F32)


def picked_rows(slot_rows, base, count, weights=None):
    wanted = iota((count, LANES), 0) + base
    parts = []
    for k in range(CHUNKS):
        hit = wanted == slot_rows[k]
        weight = 1.0 if weights is None else weights[k]
        parts.append(jnp.where(hit, weight, 0.0).astype(BF16))
    return jnp.concatenate(parts, axis=1)


def fill_message(msg_ref, slot_rows, codes_ref, tile=512):
    codes = codes_ref[...]
    for t in range(SAVED // tile):
        rows = times(picked_rows(slot_rows, t * tile, tile), codes).astype(BF16)
        first = t * tile // PAIR
        for j in range(HALVES):
            msg_ref[pl.ds(first, tile // PAIR), pl.ds(j * PAIR, PAIR), :] = rows[
                :, j * LANES : (j + 1) * LANES
            ].reshape(tile // PAIR, PAIR, LANES)


def prepare_m(target_ref, ms_ref, vs_ref, grad_ref, codes_ref, msg_ref, slot_ref):
    target = target_ref[...]
    row = lax.shift_right_logical(target, 5)
    column = target & (D // BLOCK - 1)
    dest = lax.shift_right_logical(row, 9) * N_TP + lax.shift_right_logical(column, 2)
    place = (column & (COLB - 1)) * ROWS + (row & (ROWS - 1))
    values = (
        lax.shift_right_logical(place, 7).astype(F32),
        (place & (LANES - 1)).astype(F32),
        ms_ref[...].astype(F32),
        vs_ref[...].astype(F32),
    )
    before = one_hot(iota((LANES, 2 * LANES), 0) < iota((LANES, 2 * LANES), 1))
    peer = iota((PEERS, LANES), 0)
    carry = jnp.zeros((PEERS, LANES), F32)
    side = jnp.zeros((PEERS, LANES), F32)
    slot_rows = []
    for k in range(CHUNKS):
        dest_row = dest[k : k + 1, :]
        hit = peer == dest_row
        counts = times(one_hot(hit), before)
        ahead = counts[:, :LANES] + carry
        carry = carry + counts[:, LANES:]
        rank = jnp.sum(jnp.where(hit, ahead, 0.0), axis=0, keepdims=True).astype(jnp.int32)
        slot_row = dest_row * PAIR + rank
        slot_rows.append(slot_row)
        slot_ref[k : k + 1, :] = slot_row
        ranked = iota((PAIR, LANES), 0) == rank
        table = jnp.concatenate(
            [jnp.where(ranked, v[k : k + 1, :], 0.0) for v in values]
            + [jnp.zeros((LANES - 4 * PAIR, LANES), F32)],
            axis=0,
        ).astype(BF16)
        side = side + lax.dot_general(
            one_hot(hit), table, (((1,), (1,)), ((), ())), preferred_element_type=F32
        )
    total = jnp.zeros((PAIR, grad_ref.shape[1]), F32)
    for k in range(ROWS // PAIR):
        g = grad_ref[k * PAIR : (k + 1) * PAIR, :].astype(F32)
        total = total + g * g
    total = jnp.sum(jnp.sum(total, axis=1, keepdims=True), axis=0, keepdims=True)
    high = total.astype(BF16).astype(F32)
    middle = (total - high).astype(BF16).astype(F32)
    low = total - high - middle
    lane = iota((PEERS, LANES), 1)
    side = jnp.where(lane == 64, high, side)
    side = jnp.where(lane == 65, middle, side)
    side = jnp.where(lane == 66, low, side).astype(BF16)
    spread = one_hot(
        lax.shift_right_logical(iota((PEERS * SIDE, PEERS), 0), 3) == iota((PEERS * SIDE, PEERS), 1)
    )
    msg_ref[:, pl.ds(MSG_ROWS, SIDE), :] = (
        times(spread, side).astype(BF16).reshape(PEERS, SIDE, LANES)
    )
    fill_message(msg_ref, slot_rows, codes_ref)


def prepare_v(slot_ref, codes_ref, msg_ref):
    slot = slot_ref[...]
    fill_message(msg_ref, [slot[k : k + 1, :] for k in range(CHUNKS)], codes_ref)


def received(msg_ref):
    return jnp.concatenate(
        [
            msg_ref[:, pl.ds(j * PAIR, PAIR), :].reshape(SAVED, LANES)
            for j in range(HALVES)
        ],
        axis=1,
    )


def decode_side(msg_ref):
    raw = msg_ref[:, pl.ds(MSG_ROWS, SIDE), :].reshape(PEERS * SIDE, LANES)
    gather = one_hot(iota((PEERS, PEERS * SIDE), 1) == iota((PEERS, PEERS * SIDE), 0) * SIDE)
    side = times(gather, raw)
    lane = iota((PEERS, LANES), 1)
    own = lax.shift_right_logical(lane, 4) == (iota((PEERS, LANES), 0) & 7)
    rows = []
    for q in range(4):
        widen = one_hot(
            iota((LANES, LANES), 0) == q * PAIR + (iota((LANES, LANES), 1) & (PAIR - 1))
        )
        wide = times(side.astype(BF16), widen)
        rows.append(jnp.sum(jnp.where(own, wide, 0.0).reshape(CHUNKS, 8, LANES), axis=1))
    sums = jnp.where((lane >= 64) & (lane < 67), side, 0.0)
    square_sum = jnp.sum(jnp.sum(sums, axis=1, keepdims=True), axis=0, keepdims=True)
    root_mean = jnp.sqrt(square_sum / (LAYERS * D * D) + guard)
    factor = jnp.minimum(1.0, clip_level / root_mean)
    place = (rows[0] * LANES + rows[1]).astype(jnp.int32)
    return place, rows[2], rows[3], factor


def as_row(column, count):
    rows = []
    diagonal = iota((LANES, LANES), 0) == iota((LANES, LANES), 1)
    for k in range(count // LANES):
        part = column[k * LANES : (k + 1) * LANES, :]
        rows.append(jnp.sum(jnp.where(diagonal, part, 0.0), axis=0, keepdims=True))
    return rows[0] if len(rows) == 1 else jnp.concatenate(rows, axis=1)


def scattered(place, scales, first, count, codes):
    place_rows = [place[k : k + 1, :] for k in range(CHUNKS)]
    scale_rows = [scales[k : k + 1, :] for k in range(CHUNKS)]
    matrix = jnp.concatenate(
        [picked_rows(place_rows, c * ROWS + first, count, scale_rows) for c in range(COLB)],
        axis=0,
    )
    return times(matrix, codes)


def update_m(msg_ref, grad_ref, m_ref, large_ref, step_ref, place_ref, vs_ref, factor_ref):
    count = grad_ref.shape[0]

    @pl.when(pl.program_id(0) == 0)
    def _():
        place, m_scales, v_scales, factor = decode_side(msg_ref)
        place_ref[...] = place
        vs_ref[0:CHUNKS, :] = v_scales
        vs_ref[CHUNKS:, :] = m_scales
        factor_ref[...] = jnp.broadcast_to(factor, factor_ref.shape)

    factor = factor_ref[0:1, 0:1]
    first = pl.program_id(0) * count
    previous = scattered(
        place_ref[...], vs_ref[CHUNKS:, :], first, count, received(msg_ref)
    )
    for c in range(COLB):
        columns = pl.ds(c * BLOCK, BLOCK)
        clipped = grad_ref[:, columns].astype(F32) * factor
        m_next = beta_one * previous[c * count : (c + 1) * count, :] + (1.0 - beta_one) * clipped
        largest = jnp.max(jnp.abs(m_next), axis=1, keepdims=True)
        m_ref[:, columns] = (m_next * (1.0 / (largest + guard))).astype(BF16)
        large_ref[c : c + 1, :] = as_row(largest, count)
        step_ref[:, columns] = m_next * (learn_rate / (1.0 - beta_one**step_count))


def update_v(
    msg_ref, grad_ref, param_ref, step_ref, place_ref, vs_ref, factor_ref, new_ref, v_ref, large_ref
):
    count = grad_ref.shape[0]
    factor = factor_ref[0:1, 0:1]
    first = pl.program_id(0) * count
    previous = scattered(
        place_ref[...], vs_ref[0:CHUNKS, :], first, count, received(msg_ref)
    )
    for c in range(COLB):
        columns = pl.ds(c * BLOCK, BLOCK)
        clipped = grad_ref[:, columns].astype(F32) * factor
        v_next = (
            beta_two * previous[c * count : (c + 1) * count, :]
            + (1.0 - beta_two) * clipped * clipped
        )
        largest = jnp.max(jnp.abs(v_next), axis=1, keepdims=True)
        v_ref[:, columns] = (v_next * (1.0 / (largest + guard))).astype(BF16)
        large_ref[c : c + 1, :] = as_row(largest, count)
        root = jnp.sqrt(v_next * (1.0 / (1.0 - beta_two**step_count)))
        new_ref[:, columns] = (
            param_ref[:, columns].astype(F32) - step_ref[:, columns] / (root + adam_eps)
        ).astype(BF16)


def shaped(shape, dtype):
    return jax.ShapeDtypeStruct(shape, dtype)


def whole(shape):
    return pl.BlockSpec(shape, lambda i: (0,) * len(shape))


TILE = 128


def body(param, grad, m_codes, v_codes, m_scales, v_scales, block_target):
    grad2 = grad.reshape(ROWS, COLB * BLOCK)
    param2 = param.reshape(ROWS, COLB * BLOCK)
    message_m, slot = pl.pallas_call(
        prepare_m,
        out_shape=(
            shaped((PEERS, MSG_ROWS + SIDE, LANES), BF16),
            shaped((CHUNKS, LANES), jnp.int32),
        ),
        name="prepare_m",
        interpret=INTERPRET,
    )(
        block_target.reshape(CHUNKS, LANES),
        m_scales.reshape(CHUNKS, LANES),
        v_scales.reshape(CHUNKS, LANES),
        grad2,
        m_codes,
    )
    got_m = lax.all_to_all(message_m, FSDP_TP, split_axis=0, concat_axis=0, tiled=True)
    message_v = pl.pallas_call(
        prepare_v,
        out_shape=shaped((PEERS, MSG_ROWS, LANES), BF16),
        name="prepare_v",
        interpret=INTERPRET,
    )(slot, v_codes)
    got_v = lax.all_to_all(message_v, FSDP_TP, split_axis=0, concat_axis=0, tiled=True)
    return finish(param2, grad2, got_m, got_v)


def finish(param2, grad2, got_m, got_v):
    wide = pl.BlockSpec((TILE, COLB * BLOCK), lambda i: (i, 0))
    scale_rows = pl.BlockSpec((COLB, TILE), lambda i: (0, i))
    m_quant, m_large, step, place, scales, factor = pl.pallas_call(
        update_m,
        grid=(ROWS // TILE,),
        in_specs=[whole(got_m.shape), wide],
        out_specs=[
            wide,
            scale_rows,
            wide,
            whole((CHUNKS, LANES)),
            whole((2 * CHUNKS, LANES)),
            whole((8, LANES)),
        ],
        out_shape=(
            shaped((ROWS, COLB * BLOCK), BF16),
            shaped((COLB, ROWS), F32),
            shaped((ROWS, COLB * BLOCK), F32),
            shaped((CHUNKS, LANES), jnp.int32),
            shaped((2 * CHUNKS, LANES), F32),
            shaped((8, LANES), F32),
        ),
        name="update_m",
        interpret=INTERPRET,
    )(got_m, grad2)
    new_param, v_quant, v_large = pl.pallas_call(
        update_v,
        grid=(ROWS // TILE,),
        in_specs=[
            whole(got_v.shape),
            wide,
            wide,
            wide,
            whole((CHUNKS, LANES)),
            whole((2 * CHUNKS, LANES)),
            whole((8, LANES)),
        ],
        out_specs=[wide, wide, scale_rows],
        out_shape=(
            shaped((ROWS, COLB * BLOCK), BF16),
            shaped((ROWS, COLB * BLOCK), BF16),
            shaped((COLB, ROWS), F32),
        ),
        name="update_v",
        interpret=INTERPRET,
    )(got_v, grad2, param2, step, place, scales, factor)
    return (
        new_param[None],
        m_quant[None],
        m_large.T[None],
        v_quant[None],
        v_large.T[None],
    )


def solution(mesh):
    torus = Mesh(
        mesh.devices.reshape(4, 2, 2, 4, 2), ("fsdp_0", "fsdp_1", "fsdp_2", "tp_0", "tp_1")
    )
    placed = (
        P(None, FSDP, TP),
        P(None, FSDP, TP),
        P(FSDP_TP, None),
        P(FSDP_TP, None),
        P(FSDP_TP),
        P(FSDP_TP),
        P(FSDP_TP),
    )
    return jax.shard_map(
        body,
        mesh=torus,
        in_specs=placed,
        out_specs=(
            P(None, FSDP, TP),
            P(None, FSDP, TP),
            P(None, FSDP, TP),
            P(None, FSDP, TP),
            P(None, FSDP, TP),
        ),
        check_vma=False,
    )
```

time: 173 us -> 71.6 us (0.41); the launches traced: 170 us -> 71.1 us
  local copies, waits for them, and re-layouts: 66.2 us -> 0.99 us
  blocking collectives: 53.7 us -> 0 us
  waiting for transfers between devices: 0.01 us -> 28.6 us
  other arithmetic: 27.3 us -> 0 us
  Pallas kernels: 0 us -> 24.4 us
  starting transfers between devices: 21.2 us -> 16.5 us
    psum x5 -> x0, blocking collectives: 53.7 us -> none  [by_axis(): return functools.reduce(lax.psum, axes, shard)]
    all_to_all x2, waiting for transfers between devices: 0.01 us -> 28.6 us  [the longest x1 16.5 us: body(): lax.all_to_all(message_m, FSDP_TP, split_axis=0, concat_axis=0, tiled=True)]
    gather x3 -> x0, local copies, waits for them, and re-layouts: 27.1 us -> none  [the longest x1 11.8 us: body(): positions = jnp.take(position, ordering, axis=0)]
    pallas_call x0 -> x4, Pallas kernels: none -> 24.4 us  [the longest x1 7.11 us: finish(): pl.pallas_call(update_v, grid=(ROWS // TILE,), in_specs=[whole(got_v.shap...]
    scatter x2 -> x0, local copies, waits for them, and re-layouts: 17.6 us -> none  [the longest x1 11.5 us: body(): jnp.zeros((saved_count, 2 * BLOCK), jnp.bfloat16).at[recv_places]]
    mul x3 -> x0, local copies, waits for them, and re-layouts: 8.69 us -> none  [the longest x1 3.01 us: body(): v_next = beta_two * v_prev + (1.0 - beta_two) * clipped * clipped]
    convert_element_type x2 -> x0, other arithmetic: 7.08 us -> none  [the longest x1 7.01 us: requantize(): quantized = (values / (largest[..., None] + guard)).astype(jnp.bfloat16)]
    div x4 -> x0, local copies, waits for them, and re-layouts: 5.42 us -> none  [requantize(): quantized = (values / (largest[..., None] + guard)).astype(jnp.bfloat16)]
  transfers between devices with their start and end apart: 2 -> 2, of which waited for: 0 -> 2; matrix products, arithmetic and copies ran while one was open for 18% -> 0% of each run, Pallas kernels for 0% -> 15%
where the time goes in v1:
time: 71.6 us; the launch traced here: 71.1 us
  waiting for transfers between devices  28.6 us (40%)
  Pallas kernels  24.4 us (34%)
  starting transfers between devices  16.5 us (23%)
  local copies, waits for them, and re-layouts  0.99 us (1%)
    all_to_all x1, waiting for transfers between devices, body(): lax.all_to_all(message_m, FSDP_TP, split_axis=0, concat_axis=0, tiled=True)  16.5 us
    all_to_all x1, waiting for transfers between devices, body(): lax.all_to_all(message_v, FSDP_TP, split_axis=0, concat_axis=0, tiled=True)  12.1 us
    all_to_all x1, starting transfers between devices, body(): lax.all_to_all(message_m, FSDP_TP, split_axis=0, concat_axis=0, tiled=True)  11.5 us
    pallas_call x1, Pallas kernels, finish(): pl.pallas_call(update_v, grid=(ROWS // TILE,), in_specs=[whole(got_v.shap...  7.11 us
    pallas_call x1, Pallas kernels, finish(): pl.pallas_call(update_m, grid=(ROWS // TILE,), in_specs=[whole(got_m.shap...  6.44 us
    pallas_call x1, Pallas kernels, body(): pl.pallas_call(prepare_m, out_shape=(shaped((PEERS, MSG_ROWS + SIDE, LANE...  6.27 us
    all_to_all x1, starting transfers between devices, body(): lax.all_to_all(message_v, FSDP_TP, split_axis=0, concat_axis=0, tiled=True)  5.03 us
    pallas_call x1, Pallas kernels, body(): pl.pallas_call(prepare_v, out_shape=shaped((PEERS, MSG_ROWS, LANES), BF16...  4.54 us
  transfers between devices with their start and end apart: 2, of which 2 were waited for; matrix products, arithmetic and copies ran while one was open for 0% of the time, Pallas kernels for 15%

profile of v1, /device:TPU:1, one launch (start us, length us, event | category | flops | bytes accessed | tf_op | source)
XLA Modules:
  0.0 71.1 jit_solution(6118033211217795972)
XLA Ops:
  0.6 6.3 %prepare_m.1 = (bf16[128,40,128]{2,1,0:T(8,128)(2,1)}, s32[16,128]{1,0:T(8,128)}) custom-call(s32[16,128]{1,0:T(8,128)} %bitcast.18, bf16[16,128]{1,0:T(8,128)(2,1)} %bitcast.19, bf16[16,128]{1,0:T(8,128)(2,1)} %bitcast.20, bf16[512,1024]{1,0:T(8,128)(2,1)} %bitcast.14, bf16[2048,256]{1,0:T(8,128)(2,1)} %codes_ref.2), custom_call_target="tpu_custom_call" | custom-call | tf_op jit(solution)/shard_map/prepare_m/pallas_call | solution.py:253
  6.9 11.5 %all-to-all-start.1 = ((bf16[128,40,128]{2,1,0:T(8,128)(2,1)}), bf16[128,40,128]{2,1,0:T(8,128)(2,1)S(1)}, u32[]{:S(2)}, u32[]{:S(2)}) async-start(bf16[128,40,128]{2,1,0:T(8,128)(2,1)} %get-tuple-element.17), calls=%async_computation.1 | async-start | bytes 2621440 | tf_op jit(solution)/shard_map/all_to_all | solution.py:268
  18.4 4.5 %prepare_v.1 = bf16[128,32,128]{2,1,0:T(8,128)(2,1)} custom-call(s32[16,128]{1,0:T(8,128)} %get-tuple-element.16.slot_ref, bf16[2048,256]{1,0:T(8,128)(2,1)} %codes_ref.3), custom_call_target="tpu_custom_call" | custom-call | tf_op jit(solution)/shard_map/prepare_v/pallas_call | solution.py:269
  22.9 16.5 %all-to-all-done.1.msg_ref = bf16[128,40,128]{2,1,0:T(8,128)(2,1)S(1)} async-done(((bf16[128,40,128]{2,1,0:T(8,128)(2,1)}), bf16[128,40,128]{2,1,0:T(8,128)(2,1)S(1)}, u32[]{:S(2)}, u32[]{:S(2)}) %all-to-all-start.1) | async-done | bytes 1310752 | tf_op jit(solution)/shard_map/all_to_all | solution.py:268
  39.4 0.0 copy-start
  39.4 5.0 %all-to-all-start = ((bf16[128,32,128]{2,1,0:T(8,128)(2,1)}), bf16[128,32,128]{2,1,0:T(8,128)(2,1)S(1)}, u32[]{:S(2)}, u32[]{:S(2)}) async-start(bf16[128,32,128]{2,1,0:T(8,128)(2,1)} %prepare_v.1), calls=%async_computation | async-start | bytes 2097152 | tf_op jit(solution)/shard_map/all_to_all | solution.py:275
  44.5 0.0 copy-done
  44.5 6.4 %update_m.1 = (bf16[512,1024]{1,0:T(8,128)(2,1)}, f32[4,512]{1,0:T(4,128)}, f32[512,1024]{1,0:T(8,128)}, s32[16,128]{1,0:T(8,128)}, f32[32,128]{1,0:T(8,128)}, /*index=5*/f32[8,128]{1,0:T(8,128)}) custom-call(bf16[128,40,128]{2,1,0:T(8,128)(2,1)} %copy-done, bf16[512,1024]{1,0:T(8,128)(2,1)} %bitcast.15), custom_call_target="tpu_custom_call" | custom-call | tf_op jit(solution)/shard_map/update_m/pallas_call | solution.py:282
  50.9 12.1 %all-to-all-done.msg_ref = bf16[128,32,128]{2,1,0:T(8,128)(2,1)S(1)} async-done(((bf16[128,32,128]{2,1,0:T(8,128)(2,1)}), bf16[128,32,128]{2,1,0:T(8,128)(2,1)S(1)}, u32[]{:S(2)}, u32[]{:S(2)}) %all-to-all-start) | async-done | bytes 1048608 | tf_op jit(solution)/shard_map/all_to_all | solution.py:275
  63.0 0.0 copy-start.1
  63.0 1.0 %copy-done.1 = bf16[128,32,128]{2,1,0:T(8,128)(2,1)} copy-done((bf16[128,32,128]{2,1,0:T(8,128)(2,1)}, bf16[128,32,128]{2,1,0:T(8,128)(2,1)S(1)}, u32[]{:S(2)}) %copy-start.1) | copy-done | bytes 1048600
  64.0 7.1 %update_v.1 = (bf16[512,1024]{1,0:T(8,128)(2,1)}, bf16[512,1024]{1,0:T(8,128)(2,1)}, f32[4,512]{1,0:T(4,128)}) custom-call(bf16[128,32,128]{2,1,0:T(8,128)(2,1)} %copy-done.1, bf16[512,1024]{1,0:T(8,128)(2,1)} %bitcast.16, bf16[512,1024]{1,0:T(8,128)(2,1)} %bitcast.17, f32[512,1024]{1,0:T(8,128)} %get-tuple-element.18.step_ref, ...), custom_call_target="tpu_custom_call" | custom-call | tf_op jit(solution)/shard_map/update_v/pallas_call | solution.py:305
Async XLA Ops:
  6.9 32.5 %all-to-all-start.1 = ((bf16[128,40,128]{2,1,0:T(8,128)(2,1)}), bf16[128,40,128]{2,1,0:T(8,128)(2,1)S(1)}, u32[]{:S(2)}, u32[]{:S(2)}) async-start(bf16[128,40,128]{2,1,0:T(8,128)(2,1)} %get-tuple-element.17), calls=%async_computation.1 | async-start | bytes 2621440 | tf_op jit(solution)/shard_map/all_to_all | solution.py:268
  39.4 5.0 %copy-start = (bf16[128,40,128]{2,1,0:T(8,128)(2,1)}, bf16[128,40,128]{2,1,0:T(8,128)(2,1)S(1)}, u32[]{:S(2)}) copy-start(bf16[128,40,128]{2,1,0:T(8,128)(2,1)S(1)} %all-to-all-done.1.msg_ref) | copy-start | bytes 3932164
  39.4 23.6 %all-to-all-start = ((bf16[128,32,128]{2,1,0:T(8,128)(2,1)}), bf16[128,32,128]{2,1,0:T(8,128)(2,1)S(1)}, u32[]{:S(2)}, u32[]{:S(2)}) async-start(bf16[128,32,128]{2,1,0:T(8,128)(2,1)} %prepare_v.1), calls=%async_computation | async-start | bytes 2097152 | tf_op jit(solution)/shard_map/all_to_all | solution.py:275
  63.0 1.0 %copy-start.1 = (bf16[128,32,128]{2,1,0:T(8,128)(2,1)}, bf16[128,32,128]{2,1,0:T(8,128)(2,1)S(1)}, u32[]{:S(2)}) copy-start(bf16[128,32,128]{2,1,0:T(8,128)(2,1)S(1)} %all-to-all-done.msg_ref) | copy-start | bytes 3145732

commit v2 on v1

v2 whole, which is shorter than its diff:
```python
import functools

import jax
import jax.numpy as jnp
from jax import lax
from jax.experimental import pallas as pl
from jax.experimental.pallas import tpu as pltpu
from jax.sharding import Mesh
from jax.sharding import PartitionSpec as P

D = 8192
LAYERS = 1
BLOCK = 256
FSDP = ("fsdp_0", "fsdp_1", "fsdp_2")
TP = ("tp_0", "tp_1")
FSDP_TP = ("fsdp_0", "fsdp_1", "fsdp_2", "tp_0", "tp_1")
SIZES = {"fsdp_0": 4, "fsdp_1": 2, "fsdp_2": 2, "tp_0": 4, "tp_1": 2}
EXCHANGE = ("fsdp_2", "fsdp_1", "tp_1", "tp_0", "fsdp_0")

PEERS = 128
PAIR = 16
SAVED = 2048
ROWS = 512
COLB = 4
LANES = 128
CHUNKS = SAVED // LANES
HALVES = BLOCK // LANES
MSG_ROWS = 2 * PAIR * HALVES
SIDE = 8
VMEM_LIMIT = 32 * 1024 * 1024

beta_one = 0.9
beta_two = 0.999
step_count = 1000.0
learn_rate = 0.002
clip_level = 0.5
guard = 1e-06
adam_eps = 1e-08

F32 = jnp.float32
BF16 = jnp.bfloat16


def iota(shape, dim):
    return lax.broadcasted_iota(jnp.int32, shape, dim)


def one_hot(condition):
    return jnp.where(condition, 1.0, 0.0).astype(BF16)


def times(a, b):
    return jnp.dot(a, b, preferred_element_type=F32)


def exchange_rank(fsdp, tp):
    place = {}
    for axes, index in ((FSDP, fsdp), (TP, tp)):
        for axis in reversed(axes):
            place[axis] = index & (SIZES[axis] - 1)
            index = lax.shift_right_logical(index, SIZES[axis].bit_length() - 1)
    rank = jnp.zeros_like(fsdp)
    for axis in EXCHANGE:
        rank = rank * SIZES[axis] + place[axis]
    return rank


def picked_rows(slot_rows, base, count, weights=None):
    wanted = iota((count, LANES), 0).astype(F32).astype(BF16)
    parts = []
    for k in range(CHUNKS):
        hit = wanted == (slot_rows[k] - base).astype(BF16)
        weight = jnp.ones((1, LANES), BF16) if weights is None else weights[k].astype(BF16)
        parts.append(jnp.where(hit, weight, jnp.zeros((1, LANES), BF16)))
    return jnp.concatenate(parts, axis=1)


def fill_message(msg_ref, slot_rows, m_codes, v_codes, tile=256):
    for t in range(SAVED // tile):
        matrix = picked_rows(slot_rows, float(t * tile), tile)
        first = t * tile // PAIR
        for part, codes in enumerate((m_codes, v_codes)):
            rows = times(matrix, codes).astype(BF16)
            for j in range(HALVES):
                msg_ref[
                    pl.ds(first, tile // PAIR), pl.ds((part * HALVES + j) * PAIR, PAIR), :
                ] = rows[:, j * LANES : (j + 1) * LANES].reshape(tile // PAIR, PAIR, LANES)


def prepare(target_hbm, ms_hbm, vs_hbm, grad_hbm, m_hbm, v_hbm, msg_ref, *scratch):
    refs, sem = scratch[:-1], scratch[-1]
    copies = [
        pltpu.make_async_copy(source, ref, sem.at[k])
        for k, (source, ref) in enumerate(
            zip((target_hbm, ms_hbm, vs_hbm, m_hbm, v_hbm, grad_hbm), refs)
        )
    ]
    for copy in copies:
        copy.start()
    target_ref, ms_ref, vs_ref, m_ref, v_ref, grad_ref = refs
    for copy in copies[:3]:
        copy.wait()
    target = target_ref[...]
    row = lax.shift_right_logical(target, 5)
    column = target & (D // BLOCK - 1)
    dest = exchange_rank(
        lax.shift_right_logical(row, 9), lax.shift_right_logical(column, 2)
    ).astype(F32)
    place = (column & (COLB - 1)) * ROWS + (row & (ROWS - 1))
    values = (
        lax.shift_right_logical(place, 7).astype(F32),
        (place & (LANES - 1)).astype(F32),
        ms_ref[...].astype(F32),
        vs_ref[...].astype(F32),
    )
    before = one_hot(iota((LANES, 2 * LANES), 0) < iota((LANES, 2 * LANES), 1))
    peer = iota((PEERS, LANES), 0).astype(F32)
    nth = iota((PAIR, LANES), 0).astype(F32)
    carry = jnp.zeros((PEERS, LANES), F32)
    side = jnp.zeros((PEERS, LANES), F32)
    slot_rows = []
    for k in range(CHUNKS):
        dest_row = dest[k : k + 1, :]
        hit = peer == dest_row
        hot = one_hot(hit)
        counts = times(hot, before)
        ahead = counts[:, :LANES] + carry
        carry = carry + counts[:, LANES:]
        rank = jnp.sum(jnp.where(hit, ahead, 0.0), axis=0, keepdims=True)
        slot_rows.append(dest_row * PAIR + rank)
        ranked = nth == rank
        table = jnp.concatenate(
            [jnp.where(ranked, v[k : k + 1, :], 0.0) for v in values]
            + [jnp.zeros((LANES - 4 * PAIR, LANES), F32)],
            axis=0,
        ).astype(BF16)
        side = side + lax.dot_general(
            hot, table, (((1,), (1,)), ((), ())), preferred_element_type=F32
        )
    for copy in copies[3:]:
        copy.wait()
    fill_message(msg_ref, slot_rows, m_ref[...], v_ref[...])
    total = jnp.zeros((PAIR, grad_ref.shape[1]), F32)
    for k in range(ROWS // PAIR):
        g = grad_ref[k * PAIR : (k + 1) * PAIR, :].astype(F32)
        total = total + g * g
    total = jnp.sum(jnp.sum(total, axis=1, keepdims=True), axis=0, keepdims=True)
    high = total.astype(BF16).astype(F32)
    middle = (total - high).astype(BF16).astype(F32)
    low = total - high - middle
    lane = iota((PEERS, LANES), 1)
    side = jnp.where(lane == 64, high, side)
    side = jnp.where(lane == 65, middle, side)
    side = jnp.where(lane == 66, low, side).astype(BF16)
    spread = one_hot(
        lax.shift_right_logical(iota((PEERS * SIDE, PEERS), 0), 3) == iota((PEERS * SIDE, PEERS), 1)
    )
    msg_ref[:, pl.ds(MSG_ROWS, SIDE), :] = (
        times(spread, side).astype(BF16).reshape(PEERS, SIDE, LANES)
    )


def received(msg_ref, part):
    return jnp.concatenate(
        [
            msg_ref[:, pl.ds((part * HALVES + j) * PAIR, PAIR), :].reshape(SAVED, LANES)
            for j in range(HALVES)
        ],
        axis=1,
    )


def decode_side(msg_ref):
    raw = msg_ref[:, pl.ds(MSG_ROWS, SIDE), :].reshape(PEERS * SIDE, LANES)
    gather = one_hot(iota((PEERS, PEERS * SIDE), 1) == iota((PEERS, PEERS * SIDE), 0) * SIDE)
    side = times(gather, raw)
    lane = iota((PEERS, LANES), 1)
    own = lax.shift_right_logical(lane, 4) == (iota((PEERS, LANES), 0) & 7)
    rows = []
    for q in range(4):
        widen = one_hot(
            iota((LANES, LANES), 0) == q * PAIR + (iota((LANES, LANES), 1) & (PAIR - 1))
        )
        wide = times(side.astype(BF16), widen)
        rows.append(jnp.sum(jnp.where(own, wide, 0.0).reshape(CHUNKS, 8, LANES), axis=1))
    sums = jnp.where((lane >= 64) & (lane < 67), side, 0.0)
    square_sum = jnp.sum(jnp.sum(sums, axis=1, keepdims=True), axis=0, keepdims=True)
    root_mean = jnp.sqrt(square_sum / (LAYERS * D * D) + guard)
    factor = jnp.minimum(1.0, clip_level / root_mean)
    place = rows[0] * LANES + rows[1]
    return place, rows[2], rows[3], factor


def as_row(column, count):
    rows = []
    diagonal = iota((LANES, LANES), 0) == iota((LANES, LANES), 1)
    for k in range(count // LANES):
        part = column[k * LANES : (k + 1) * LANES, :]
        rows.append(jnp.sum(jnp.where(diagonal, part, 0.0), axis=0, keepdims=True))
    return rows[0] if len(rows) == 1 else jnp.concatenate(rows, axis=1)


def scattered(place, scales, first, count, codes):
    place_rows = [place[k : k + 1, :] for k in range(CHUNKS)]
    scale_rows = [scales[k : k + 1, :] for k in range(CHUNKS)]
    matrix = jnp.concatenate(
        [
            picked_rows(place_rows, (c * ROWS + first).astype(F32), count, scale_rows)
            for c in range(COLB)
        ],
        axis=0,
    )
    return times(matrix, codes)


def update(
    msg_ref, grad_ref, param_ref, new_ref, m_ref, ml_ref, v_ref, vl_ref, place_ref, scale_ref, factor_ref
):
    count = new_ref.shape[0]

    @pl.when(pl.program_id(0) == 0)
    def _():
        place, m_scales, v_scales, factor = decode_side(msg_ref)
        place_ref[...] = place
        scale_ref[0, :, :] = m_scales
        scale_ref[1, :, :] = v_scales
        factor_ref[...] = jnp.broadcast_to(factor, factor_ref.shape)

    factor = factor_ref[0:1, 0:1]
    first = pl.program_id(0) * count
    place = place_ref[...]
    here = pl.ds(pl.multiple_of(first, count), count)
    m_prev = scattered(place, scale_ref[0, :, :], first, count, received(msg_ref, 0))
    v_prev = scattered(place, scale_ref[1, :, :], first, count, received(msg_ref, 1))
    for c in range(COLB):
        columns = pl.ds(c * BLOCK, BLOCK)
        part = slice(c * count, (c + 1) * count)
        clipped = grad_ref[here, columns].astype(F32) * factor
        m_next = beta_one * m_prev[part, :] + (1.0 - beta_one) * clipped
        largest = jnp.max(jnp.abs(m_next), axis=1, keepdims=True)
        m_ref[:, columns] = (m_next * (1.0 / (largest + guard))).astype(BF16)
        ml_ref[c : c + 1, :] = as_row(largest, count)
        v_next = beta_two * v_prev[part, :] + (1.0 - beta_two) * clipped * clipped
        largest = jnp.max(jnp.abs(v_next), axis=1, keepdims=True)
        v_ref[:, columns] = (v_next * (1.0 / (largest + guard))).astype(BF16)
        vl_ref[c : c + 1, :] = as_row(largest, count)
        root = jnp.sqrt(v_next * (1.0 / (1.0 - beta_two**step_count)))
        step = m_next * (learn_rate / (1.0 - beta_one**step_count)) / (root + adam_eps)
        new_ref[:, columns] = (param_ref[here, columns].astype(F32) - step).astype(BF16)


def shaped(shape, dtype):
    return jax.ShapeDtypeStruct(shape, dtype)


def whole(shape):
    return pl.BlockSpec(shape, lambda i: (0,) * len(shape))


TILE = 128


def make_message(grad2, m_codes, v_codes, m_scales, v_scales, block_target):
    arrays = (
        block_target.reshape(CHUNKS, LANES),
        m_scales.reshape(CHUNKS, LANES),
        v_scales.reshape(CHUNKS, LANES),
        grad2,
        m_codes,
        v_codes,
    )
    held = [arrays[k] for k in (0, 1, 2, 4, 5, 3)]
    return pl.pallas_call(
        prepare,
        in_specs=[pl.BlockSpec(memory_space=pltpu.HBM)] * len(arrays),
        out_shape=pltpu.VMEM((PEERS, MSG_ROWS + SIDE, LANES), BF16),
        scratch_shapes=[pltpu.VMEM(a.shape, a.dtype) for a in held]
        + [pltpu.SemaphoreType.DMA((len(held),))],
        name="prepare",
        compiler_params=pltpu.CompilerParams(vmem_limit_bytes=VMEM_LIMIT),
    )(*(pltpu.with_memory_space_constraint(a, pltpu.HBM) for a in arrays))


def finish(got, grad2, param2):
    wide = pl.BlockSpec((TILE, COLB * BLOCK), lambda i: (i, 0))
    scale_rows = pl.BlockSpec((COLB, TILE), lambda i: (0, i))
    matrix = shaped((ROWS, COLB * BLOCK), BF16)
    scales = shaped((COLB, ROWS), F32)
    return pl.pallas_call(
        update,
        grid=(ROWS // TILE,),
        in_specs=[pl.BlockSpec(memory_space=pltpu.VMEM)] * 3,
        out_specs=[wide, wide, scale_rows, wide, scale_rows],
        out_shape=(matrix, matrix, scales, matrix, scales),
        scratch_shapes=[
            pltpu.VMEM((CHUNKS, LANES), F32),
            pltpu.VMEM((2, CHUNKS, LANES), F32),
            pltpu.VMEM((8, LANES), F32),
        ],
        name="update",
        compiler_params=pltpu.CompilerParams(vmem_limit_bytes=VMEM_LIMIT),
    )(*(pltpu.with_memory_space_constraint(a, pltpu.VMEM) for a in (got, grad2, param2)))


def body(param, grad, m_codes, v_codes, m_scales, v_scales, block_target):
    grad2 = grad.reshape(ROWS, COLB * BLOCK)
    param2 = param.reshape(ROWS, COLB * BLOCK)
    message = make_message(grad2, m_codes, v_codes, m_scales, v_scales, block_target)
    got = lax.all_to_all(message, EXCHANGE, split_axis=0, concat_axis=0, tiled=True)
    new_param, m_quant, m_large, v_quant, v_large = finish(got, grad2, param2)
    return (
        new_param[None],
        m_quant[None],
        m_large.T[None],
        v_quant[None],
        v_large.T[None],
    )


def solution(mesh):
    torus = Mesh(
        mesh.devices.reshape(4, 2, 2, 4, 2), ("fsdp_0", "fsdp_1", "fsdp_2", "tp_0", "tp_1")
    )
    placed = (
        P(None, FSDP, TP),
        P(None, FSDP, TP),
        P(FSDP_TP, None),
        P(FSDP_TP, None),
        P(FSDP_TP),
        P(FSDP_TP),
        P(FSDP_TP),
    )
    return jax.shard_map(
        body,
        mesh=torus,
        in_specs=placed,
        out_specs=(
            P(None, FSDP, TP),
            P(None, FSDP, TP),
            P(None, FSDP, TP),
            P(None, FSDP, TP),
            P(None, FSDP, TP),
        ),
        check_vma=False,
    )
```

time: 71.6 us -> 58.4 us (0.82)
  blocking collectives: 0 us -> 42.6 us
  waiting for transfers between devices: 28.6 us -> 0 us
  starting transfers between devices: 16.5 us -> 0 us
  Pallas kernels: 24.4 us -> 14.9 us
  local copies, waits for them, and re-layouts: 0.99 us -> 0.01 us
    all_to_all x0 -> x1, blocking collectives: none -> 42.6 us  [body(): lax.all_to_all(message, EXCHANGE, split_axis=0, concat_axis=0, tiled=True)]
    all_to_all x2 -> x0, waiting for transfers between devices: 28.6 us -> none  [the longest x1 16.5 us: body(): lax.all_to_all(message_m, FSDP_TP, split_axis=0, concat_axis=0, tiled=True)]
    all_to_all x2 -> x0, starting transfers between devices: 16.5 us -> none  [the longest x1 11.5 us: body(): lax.all_to_all(message_m, FSDP_TP, split_axis=0, concat_axis=0, tiled=True)]
    pallas_call x4 -> x2, Pallas kernels: 24.4 us -> 14.9 us  [the longest x1 8.29 us: finish(): pl.pallas_call(update, grid=(ROWS // TILE,), in_specs=[pl.BlockSpec(memor...]
    unnamed x4, local copies, waits for them, and re-layouts: 0.99 us -> 0.01 us
  transfers between devices with their start and end apart: 2 -> 0, of which waited for: 2 -> 0; matrix products, arithmetic and copies ran while one was open for 0% -> 0% of each run, Pallas kernels for 15% -> 0%
where the time goes in v2:
time: 58.4 us; the launch traced here: 58.2 us
  blocking collectives  42.6 us (73%)
  Pallas kernels  14.9 us (26%)
  between operations  0.66 us (1%)
    all_to_all x1, blocking collectives, body(): lax.all_to_all(message, EXCHANGE, split_axis=0, concat_axis=0, tiled=True)  42.6 us
    pallas_call x1, Pallas kernels, finish(): pl.pallas_call(update, grid=(ROWS // TILE,), in_specs=[pl.BlockSpec(memor...  8.29 us
    pallas_call x1, Pallas kernels, make_message(): pl.pallas_call(prepare, in_specs=[pl.BlockSpec(memory_space=pltpu.HBM)] *...  6.61 us

profile of v2, /device:TPU:1, one launch (start us, length us, event | category | flops | bytes accessed | tf_op | source)
XLA Modules:
  0.0 58.2 jit_solution(15139146320575948800)
XLA Ops:
  0.6 6.6 %prepare.1 = bf16[128,72,128]{2,1,0:T(8,128)(2,1)S(1)} custom-call(s32[16,128]{1,0:T(8,128)} %bitcast.17, bf16[16,128]{1,0:T(8,128)(2,1)} %bitcast.18, bf16[16,128]{1,0:T(8,128)(2,1)} %bitcast.19, bf16[512,1024]{1,0:T(8,128)(2,1)} %bitcast.14, bf16[2048,256]{1,0:T(8,128)(2,1)} %m_hbm.1, bf16[2048,256]{1,0:T(8,128)(2,1)} %v_hbm.1), custom_call_target="tpu_custom_call" | custom-call | tf_op jit(solution)/shard_map/prepare/pallas_call | solution.py:273
  7.2 0.0 copy-start
  7.3 0.0 copy-start.1
  7.3 42.6 %all_to_all.5.msg_ref = bf16[128,72,128]{2,1,0:T(8,128)(2,1)S(1)} all-to-all(bf16[128,72,128]{2,1,0:T(8,128)(2,1)S(1)} %prepare.1), channel_id=1, replica_groups=mesh['fsdp_0'=4,'fsdp_1'=2,'fsdp_2'=2,'tp_0'=4,'tp_1'=2] {'fsdp_2','fsdp..., dimensions={0} | all-to-all | bytes 4718592 | tf_op jit(solution)/shard_map/all_to_all | solution.py:309
  49.9 0.0 copy-done
  49.9 0.0 copy-done.1
  49.9 8.3 %update.1 = (bf16[512,1024]{1,0:T(8,128)(2,1)}, bf16[512,1024]{1,0:T(8,128)(2,1)}, f32[4,512]{1,0:T(4,128)}, bf16[512,1024]{1,0:T(8,128)(2,1)}, f32[4,512]{1,0:T(4,128)}) custom-call(bf16[128,72,128]{2,1,0:T(8,128)(2,1)S(1)} %all_to_all.5.msg_ref, bf16[512,1024]{1,0:T(8,128)(2,1)S(1)} %bitcast.15, bf16[512,1024]{1,0:T(8,128)(2,1)S(1)} %bitcast.16), custom_call_target="tpu_custom_call" | custom-call | tf_op jit(solution)/shard_map/update/pallas_call | solution.py:289
Async XLA Ops:
  7.2 42.7 %copy-start = (bf16[1,512,1024]{2,1,0:T(8,128)(2,1)S(1)}, bf16[1,512,1024]{2,1,0:T(8,128)(2,1)}, u32[]{:S(2)}) copy-start(bf16[1,512,1024]{2,1,0:T(8,128)(2,1)} %param.8) | copy-start | bytes 3145732
  7.3 42.6 %copy-start.1 = (bf16[1,512,1024]{2,1,0:T(8,128)(2,1)S(1)}, bf16[1,512,1024]{2,1,0:T(8,128)(2,1)}, u32[]{:S(2)}) copy-start(bf16[1,512,1024]{2,1,0:T(8,128)(2,1)} %param.7) | copy-start | bytes 3145732

commit v3 on v2

--- a/solution.py
+++ b/solution.py
@@ -26,7 +26,8 @@
 CHUNKS = SAVED // LANES
 HALVES = BLOCK // LANES
 MSG_ROWS = 2 * PAIR * HALVES
-SIDE = 8
+SIDE = 2
+STRIDE = MSG_ROWS + SIDE
 VMEM_LIMIT = 32 * 1024 * 1024
 
 beta_one = 0.9
@@ -70,21 +71,29 @@
     parts = []
     for k in range(CHUNKS):
         hit = wanted == (slot_rows[k] - base).astype(BF16)
-        weight = jnp.ones((1, LANES), BF16) if weights is None else weights[k].astype(BF16)
+        weight = jnp.ones((1, LANES), BF16) if weights is None else weights[k]
         parts.append(jnp.where(hit, weight, jnp.zeros((1, LANES), BF16)))
     return jnp.concatenate(parts, axis=1)
 
 
-def fill_message(msg_ref, slot_rows, m_codes, v_codes, tile=256):
+def fill_message(msg_ref, slot_rows, m_codes, v_codes, tile=512, step=256):
     for t in range(SAVED // tile):
-        matrix = picked_rows(slot_rows, float(t * tile), tile)
+        matrix = jnp.concatenate(
+            [
+                picked_rows(slot_rows, float(base), step)
+                for base in range(t * tile, (t + 1) * tile, step)
+            ],
+            axis=0,
+        )
         first = t * tile // PAIR
         for part, codes in enumerate((m_codes, v_codes)):
             rows = times(matrix, codes).astype(BF16)
             for j in range(HALVES):
-                msg_ref[
-                    pl.ds(first, tile // PAIR), pl.ds((part * HALVES + j) * PAIR, PAIR), :
-                ] = rows[:, j * LANES : (j + 1) * LANES].reshape(tile // PAIR, PAIR, LANES)
+                for p in range(tile // PAIR):
+                    at = (first + p) * STRIDE + (part * HALVES + j) * PAIR
+                    msg_ref[at : at + PAIR, :] = rows[
+                        p * PAIR : (p + 1) * PAIR, j * LANES : (j + 1) * LANES
+                    ]
 
 
 def prepare(target_hbm, ms_hbm, vs_hbm, grad_hbm, m_hbm, v_hbm, msg_ref, *scratch):
@@ -92,12 +101,12 @@
     copies = [
         pltpu.make_async_copy(source, ref, sem.at[k])
         for k, (source, ref) in enumerate(
-            zip((target_hbm, ms_hbm, vs_hbm, m_hbm, v_hbm, grad_hbm), refs)
+            zip((target_hbm, ms_hbm, vs_hbm, grad_hbm, m_hbm, v_hbm), refs)
         )
     ]
     for copy in copies:
         copy.start()
-    target_ref, ms_ref, vs_ref, m_ref, v_ref, grad_ref = refs
+    target_ref, ms_ref, vs_ref, grad_ref, m_ref, v_ref = refs
     for copy in copies[:3]:
         copy.wait()
     target = target_ref[...]
@@ -119,7 +128,14 @@
     carry = jnp.zeros((PEERS, LANES), F32)
     side = jnp.zeros((PEERS, LANES), F32)
     slot_rows = []
+    total = jnp.zeros((8, grad_ref.shape[1]), F32)
     for k in range(CHUNKS):
+        if k == CHUNKS // 2:
+            copies[3].wait()
+        if k >= CHUNKS // 2:
+            share = 2 * ROWS // CHUNKS
+            g = grad_ref[(k - CHUNKS // 2) * share : (k - CHUNKS // 2 + 1) * share, :].astype(F32)
+            total = total + jnp.sum((g * g).reshape(-1, 8, g.shape[1]), axis=0)
         dest_row = dest[k : k + 1, :]
         hit = peer == dest_row
         hot = one_hot(hit)
@@ -137,13 +153,6 @@
         side = side + lax.dot_general(
             hot, table, (((1,), (1,)), ((), ())), preferred_element_type=F32
         )
-    for copy in copies[3:]:
-        copy.wait()
-    fill_message(msg_ref, slot_rows, m_ref[...], v_ref[...])
-    total = jnp.zeros((PAIR, grad_ref.shape[1]), F32)
-    for k in range(ROWS // PAIR):
-        g = grad_ref[k * PAIR : (k + 1) * PAIR, :].astype(F32)
-        total = total + g * g
     total = jnp.sum(jnp.sum(total, axis=1, keepdims=True), axis=0, keepdims=True)
     high = total.astype(BF16).astype(F32)
     middle = (total - high).astype(BF16).astype(F32)
@@ -153,17 +162,27 @@
     side = jnp.where(lane == 65, middle, side)
     side = jnp.where(lane == 66, low, side).astype(BF16)
     spread = one_hot(
-        lax.shift_right_logical(iota((PEERS * SIDE, PEERS), 0), 3) == iota((PEERS * SIDE, PEERS), 1)
-    )
-    msg_ref[:, pl.ds(MSG_ROWS, SIDE), :] = (
-        times(spread, side).astype(BF16).reshape(PEERS, SIDE, LANES)
-    )
+        lax.shift_right_logical(iota((PEERS * SIDE, PEERS), 0), 1) == iota((PEERS * SIDE, PEERS), 1)
+    )
+    side = times(spread, side).astype(BF16)
+    for p in range(PEERS):
+        at = p * STRIDE + MSG_ROWS
+        msg_ref[at : at + SIDE, :] = side[p * SIDE : (p + 1) * SIDE, :]
+    for copy in copies[4:]:
+        copy.wait()
+    fill_message(msg_ref, slot_rows, m_ref[...], v_ref[...])
 
 
 def received(msg_ref, part):
     return jnp.concatenate(
         [
-            msg_ref[:, pl.ds((part * HALVES + j) * PAIR, PAIR), :].reshape(SAVED, LANES)
+            jnp.concatenate(
+                [
+                    msg_ref[at : at + PAIR, :]
+                    for at in range((part * HALVES + j) * PAIR, PEERS * STRIDE, STRIDE)
+                ],
+                axis=0,
+            )
             for j in range(HALVES)
         ],
         axis=1,
@@ -171,8 +190,16 @@
 
 
 def decode_side(msg_ref):
-    raw = msg_ref[:, pl.ds(MSG_ROWS, SIDE), :].reshape(PEERS * SIDE, LANES)
-    gather = one_hot(iota((PEERS, PEERS * SIDE), 1) == iota((PEERS, PEERS * SIDE), 0) * SIDE)
+    raw = jnp.concatenate(
+        [
+            msg_ref[at : at + PAIR, :]
+            for at in range(STRIDE - PAIR, PEERS * STRIDE, STRIDE)
+        ],
+        axis=0,
+    )
+    gather = one_hot(
+        iota((PEERS, PEERS * PAIR), 1) == iota((PEERS, PEERS * PAIR), 0) * PAIR + (PAIR - SIDE)
+    )
     side = times(gather, raw)
     lane = iota((PEERS, LANES), 1)
     own = lax.shift_right_logical(lane, 4) == (iota((PEERS, LANES), 0) & 7)
@@ -200,12 +227,10 @@
     return rows[0] if len(rows) == 1 else jnp.concatenate(rows, axis=1)
 
 
-def scattered(place, scales, first, count, codes):
-    place_rows = [place[k : k + 1, :] for k in range(CHUNKS)]
-    scale_rows = [scales[k : k + 1, :] for k in range(CHUNKS)]
+def scattered(place_rows, scale_rows, first, count, codes):
     matrix = jnp.concatenate(
         [
-            picked_rows(place_rows, (c * ROWS + first).astype(F32), count, scale_rows)
+            picked_rows(place_rows, float(c * ROWS + first), count, scale_rows)
             for c in range(COLB)
         ],
         axis=0,
@@ -213,40 +238,63 @@
     return times(matrix, codes)
 
 
-def update(
-    msg_ref, grad_ref, param_ref, new_ref, m_ref, ml_ref, v_ref, vl_ref, place_ref, scale_ref, factor_ref
-):
-    count = new_ref.shape[0]
-
-    @pl.when(pl.program_id(0) == 0)
-    def _():
-        place, m_scales, v_scales, factor = decode_side(msg_ref)
-        place_ref[...] = place
-        scale_ref[0, :, :] = m_scales
-        scale_ref[1, :, :] = v_scales
-        factor_ref[...] = jnp.broadcast_to(factor, factor_ref.shape)
-
-    factor = factor_ref[0:1, 0:1]
-    first = pl.program_id(0) * count
-    place = place_ref[...]
-    here = pl.ds(pl.multiple_of(first, count), count)
-    m_prev = scattered(place, scale_ref[0, :, :], first, count, received(msg_ref, 0))
-    v_prev = scattered(place, scale_ref[1, :, :], first, count, received(msg_ref, 1))
-    for c in range(COLB):
-        columns = pl.ds(c * BLOCK, BLOCK)
-        part = slice(c * count, (c + 1) * count)
-        clipped = grad_ref[here, columns].astype(F32) * factor
-        m_next = beta_one * m_prev[part, :] + (1.0 - beta_one) * clipped
-        largest = jnp.max(jnp.abs(m_next), axis=1, keepdims=True)
-        m_ref[:, columns] = (m_next * (1.0 / (largest + guard))).astype(BF16)
-        ml_ref[c : c + 1, :] = as_row(largest, count)
-        v_next = beta_two * v_prev[part, :] + (1.0 - beta_two) * clipped * clipped
-        largest = jnp.max(jnp.abs(v_next), axis=1, keepdims=True)
-        v_ref[:, columns] = (v_next * (1.0 / (largest + guard))).astype(BF16)
-        vl_ref[c : c + 1, :] = as_row(largest, count)
-        root = jnp.sqrt(v_next * (1.0 / (1.0 - beta_two**step_count)))
-        step = m_next * (learn_rate / (1.0 - beta_one**step_count)) / (root + adam_eps)
-        new_ref[:, columns] = (param_ref[here, columns].astype(F32) - step).astype(BF16)
+def update(msg_ref, grad_ref, param_ref, *rest):
+    outs, held, sem = rest[:5], rest[5:10], rest[10]
+    new_ref, m_ref, ml_ref, v_ref, vl_ref = held
+    place, m_scales, v_scales, factor = decode_side(msg_ref)
+    place_rows = [place[k : k + 1, :] for k in range(CHUNKS)]
+    m_rows = [m_scales[k : k + 1, :].astype(BF16) for k in range(CHUNKS)]
+    v_rows = [v_scales[k : k + 1, :].astype(BF16) for k in range(CHUNKS)]
+    m_codes, v_codes = received(msg_ref, 0), received(msg_ref, 1)
+    gain = factor * (1.0 - beta_one)
+
+    def previous(first):
+        return (
+            scattered(place_rows, m_rows, first, TILE, m_codes),
+            scattered(place_rows, v_rows, first, TILE, v_codes),
+        )
+
+    def finish_tile(first, m_prev, v_prev):
+        here = pl.ds(first, TILE)
+        for c in range(COLB):
+            columns = pl.ds(c * BLOCK, BLOCK)
+            part = slice(c * TILE, (c + 1) * TILE)
+            added = grad_ref[here, columns].astype(F32) * gain
+            m_next = beta_one * m_prev[part, :] + added
+            largest = jnp.max(jnp.abs(m_next), axis=1, keepdims=True)
+            m_ref[here, columns] = (m_next * (1.0 / (largest + guard))).astype(BF16)
+            ml_ref[c : c + 1, here] = as_row(largest, TILE)
+            v_next = beta_two * v_prev[part, :] + added * added * (
+                (1.0 - beta_two) / (1.0 - beta_one) ** 2
+            )
+            largest = jnp.max(v_next, axis=1, keepdims=True)
+            v_ref[here, columns] = (v_next * (1.0 / (largest + guard))).astype(BF16)
+            vl_ref[c : c + 1, here] = as_row(largest, TILE)
+            square = v_next * (1.0 / (1.0 - beta_two**step_count))
+            root = square * lax.rsqrt(square)
+            step = m_next * (learn_rate / (1.0 - beta_one**step_count)) / (root + adam_eps)
+            new_ref[here, columns] = (param_ref[here, columns].astype(F32) - step).astype(BF16)
+
+    copies = []
+
+    def send(k, here):
+        copies.append(
+            pltpu.make_async_copy(held[k].at[here], outs[k].at[here], sem.at[len(copies)])
+        )
+        copies[-1].start()
+
+    ahead = previous(0)
+    for first in range(0, ROWS, TILE):
+        now = ahead
+        if first + TILE < ROWS:
+            ahead = previous(first + TILE)
+        finish_tile(first, *now)
+        for k in (0, 1, 3):
+            send(k, pl.ds(first, TILE))
+    for k in (2, 4):
+        send(k, pl.ds(0, COLB))
+    for copy in copies:
+        copy.wait()
 
 
 def shaped(shape, dtype):
@@ -269,34 +317,28 @@
         m_codes,
         v_codes,
     )
-    held = [arrays[k] for k in (0, 1, 2, 4, 5, 3)]
     return pl.pallas_call(
         prepare,
         in_specs=[pl.BlockSpec(memory_space=pltpu.HBM)] * len(arrays),
-        out_shape=pltpu.VMEM((PEERS, MSG_ROWS + SIDE, LANES), BF16),
-        scratch_shapes=[pltpu.VMEM(a.shape, a.dtype) for a in held]
-        + [pltpu.SemaphoreType.DMA((len(held),))],
+        out_shape=pltpu.VMEM((PEERS * STRIDE, LANES), BF16),
+        scratch_shapes=[pltpu.VMEM(a.shape, a.dtype) for a in arrays]
+        + [pltpu.SemaphoreType.DMA((len(arrays),))],
         name="prepare",
         compiler_params=pltpu.CompilerParams(vmem_limit_bytes=VMEM_LIMIT),
     )(*(pltpu.with_memory_space_constraint(a, pltpu.HBM) for a in arrays))
 
 
 def finish(got, grad2, param2):
-    wide = pl.BlockSpec((TILE, COLB * BLOCK), lambda i: (i, 0))
-    scale_rows = pl.BlockSpec((COLB, TILE), lambda i: (0, i))
-    matrix = shaped((ROWS, COLB * BLOCK), BF16)
-    scales = shaped((COLB, ROWS), F32)
+    matrix = ((ROWS, COLB * BLOCK), BF16)
+    scales = ((COLB, ROWS), F32)
+    outs = (matrix, matrix, scales, matrix, scales)
     return pl.pallas_call(
         update,
-        grid=(ROWS // TILE,),
         in_specs=[pl.BlockSpec(memory_space=pltpu.VMEM)] * 3,
-        out_specs=[wide, wide, scale_rows, wide, scale_rows],
-        out_shape=(matrix, matrix, scales, matrix, scales),
-        scratch_shapes=[
-            pltpu.VMEM((CHUNKS, LANES), F32),
-            pltpu.VMEM((2, CHUNKS, LANES), F32),
-            pltpu.VMEM((8, LANES), F32),
-        ],
+        out_specs=[pl.BlockSpec(memory_space=pltpu.HBM)] * len(outs),
+        out_shape=tuple(pltpu.HBM(*o) for o in outs),
+        scratch_shapes=[pltpu.VMEM(*o) for o in outs]
+        + [pltpu.SemaphoreType.DMA((3 * ROWS // TILE + 2,))],
         name="update",
         compiler_params=pltpu.CompilerParams(vmem_limit_bytes=VMEM_LIMIT),
     )(*(pltpu.with_memory_space_constraint(a, pltpu.VMEM) for a in (got, grad2, param2)))
@@ -306,7 +348,9 @@
     grad2 = grad.reshape(ROWS, COLB * BLOCK)
     param2 = param.reshape(ROWS, COLB * BLOCK)
     message = make_message(grad2, m_codes, v_codes, m_scales, v_scales, block_target)
-    got = lax.all_to_all(message, EXCHANGE, split_axis=0, concat_axis=0, tiled=True)
+    pairs = message.reshape(PEERS, STRIDE // 2, 2, LANES)
+    got = lax.all_to_all(pairs, EXCHANGE, split_axis=0, concat_axis=0, tiled=True)
+    got = got.reshape(PEERS * STRIDE, LANES)
     new_param, m_quant, m_large, v_quant, v_large = finish(got, grad2, param2)
     return (
         new_param[None],

time: 58.4 us -> 54.4 us (0.932)
  blocking collectives: 42.6 us -> 40.5 us
  Pallas kernels: 14.9 us -> 13.1 us
    all_to_all x1, blocking collectives: 42.6 us -> 40.5 us  [body(): lax.all_to_all(pairs, EXCHANGE, split_axis=0, concat_axis=0, tiled=True)]
    pallas_call x1, Pallas kernels: 8.29 us -> 6.42 us  [finish(): pl.pallas_call(update, in_specs=[pl.BlockSpec(memory_space=pltpu.VMEM)] *...]
where the time goes in v3:
time: 54.4 us; the launch traced here: 54.2 us
  blocking collectives  40.5 us (74%)
  Pallas kernels  13.1 us (24%)
  between operations  0.66 us (1%)
    all_to_all x1, blocking collectives, body(): lax.all_to_all(pairs, EXCHANGE, split_axis=0, concat_axis=0, tiled=True)  40.5 us
    pallas_call x1, Pallas kernels, make_message(): pl.pallas_call(prepare, in_specs=[pl.BlockSpec(memory_space=pltpu.HBM)] *...  6.67 us
    pallas_call x1, Pallas kernels, finish(): pl.pallas_call(update, in_specs=[pl.BlockSpec(memory_space=pltpu.VMEM)] *...  6.42 us

profile of v3, /device:TPU:1, one launch (start us, length us, event | category | flops | bytes accessed | tf_op | source)
XLA Modules:
  0.0 54.2 jit_solution(1205104825887058341)
XLA Ops:
  0.6 6.7 %prepare.1 = bf16[8448,128]{1,0:T(8,128)(2,1)S(1)} custom-call(s32[16,128]{1,0:T(8,128)} %bitcast.21, bf16[16,128]{1,0:T(8,128)(2,1)} %bitcast.22, bf16[16,128]{1,0:T(8,128)(2,1)} %bitcast.23, bf16[512,1024]{1,0:T(8,128)(2,1)} %bitcast.18, bf16[2048,256]{1,0:T(8,128)(2,1)} %m_hbm.1, bf16[2048,256]{1,0:T(8,128)(2,1)} %v_hbm.1), custom_call_target="tpu_custom_call" | custom-call | tf_op jit(solution)/shard_map/prepare/pallas_call | solution.py:320
  7.3 0.0 copy-start
  7.3 0.0 copy-start.1
  7.3 40.5 %all_to_all.5 = bf16[128,33,2,128]{3,2,1,0:T(2,128)(2,1)S(1)} all-to-all(bf16[128,33,2,128]{3,2,1,0:T(2,128)(2,1)S(1)} %bitcast.17), channel_id=1, replica_groups=mesh['fsdp_0'=4,'fsdp_1'=2,'fsdp_2'=2,'tp_0'=4,'tp_1'=2] {'fsdp_2','fsdp..., dimensions={0} | all-to-all | bytes 4325376 | tf_op jit(solution)/shard_map/all_to_all | solution.py:352
  47.8 0.0 copy-done
  47.8 0.0 copy-done.1
  47.8 6.4 %update.1 = (bf16[512,1024]{1,0:T(8,128)(2,1)}, bf16[512,1024]{1,0:T(8,128)(2,1)}, f32[4,512]{1,0:T(4,128)}, bf16[512,1024]{1,0:T(8,128)(2,1)}, f32[4,512]{1,0:T(4,128)}) custom-call(bf16[8448,128]{1,0:T(8,128)(2,1)S(1)} %bitcast.16, bf16[512,1024]{1,0:T(8,128)(2,1)S(1)} %bitcast.19, bf16[512,1024]{1,0:T(8,128)(2,1)S(1)} %bitcast.20), custom_call_target="tpu_custom_call" | custom-call | tf_op jit(solution)/shard_map/update/pallas_call | solution.py:335
Async XLA Ops:
  7.3 40.5 %copy-start = (bf16[1,512,1024]{2,1,0:T(8,128)(2,1)S(1)}, bf16[1,512,1024]{2,1,0:T(8,128)(2,1)}, u32[]{:S(2)}) copy-start(bf16[1,512,1024]{2,1,0:T(8,128)(2,1)} %param.8) | copy-start | bytes 3145732
  7.3 40.5 %copy-start.1 = (bf16[1,512,1024]{2,1,0:T(8,128)(2,1)S(1)}, bf16[1,512,1024]{2,1,0:T(8,128)(2,1)}, u32[]{:S(2)}) copy-start(bf16[1,512,1024]{2,1,0:T(8,128)(2,1)} %param.7) | copy-start | bytes 3145732

commit v4 on v3

--- a/solution.py
+++ b/solution.py
@@ -1,4 +1,5 @@
 import functools
+import math
 
 import jax
 import jax.numpy as jnp
@@ -38,6 +39,9 @@
 guard = 1e-06
 adam_eps = 1e-08
 
+M_UNIT = learn_rate * beta_one / (1.0 - beta_one**step_count)
+V_UNIT = math.sqrt(beta_two / (1.0 - beta_two**step_count)) / M_UNIT
+
 F32 = jnp.float32
 BF16 = jnp.bfloat16
 
@@ -76,6 +80,96 @@
     return jnp.concatenate(parts, axis=1)
 
 
+GROUP = 64
+WIDE = 2 * LANES
+TILES = SAVED // WIDE
+
+
+def paired_rows(array):
+    return paired([array[k : k + 1, :] for k in range(CHUNKS)])
+
+
+def paired(rows):
+    return jnp.concatenate(
+        [jnp.concatenate(rows[k::2], axis=0) for k in range(2)], axis=1
+    )
+
+
+def grouped(target):
+    tile = jnp.floor(target * (1.0 / WIDE))
+    nth = iota((TILES, WIDE), 0).astype(F32)
+    hit = jnp.concatenate([nth == tile[k : k + 1, :] for k in range(TILES)], axis=0)
+    before = one_hot(iota((WIDE, WIDE), 0) < iota((WIDE, WIDE), 1))
+    ahead = jnp.where(hit, times(one_hot(hit), before), 0.0)
+    rank = jnp.sum(ahead.reshape(TILES, TILES, WIDE), axis=1)
+    fits = jnp.max(rank) < GROUP - 0.5
+    return target - tile * WIDE, tile * GROUP + rank, fits
+
+
+def sort_chunks(row, labels, chunk_codes, held_ref):
+    found = []
+    for k in range(TILES):
+        step = SAVED // TILES
+        matrix = jnp.concatenate(
+            [one_level(row[k : k + 1, :], float(base)) for base in (0, step)], axis=0
+        )
+        held_ref[:, k * GROUP : (k + 1) * GROUP, :] = (
+            times(matrix, chunk_codes(k)).astype(BF16).reshape(TILES, GROUP, 2 * BLOCK)
+        )
+        table = jnp.concatenate(
+            [v[k : k + 1, :] for v in labels] + [jnp.zeros((PAIR - len(labels), WIDE), F32)], axis=0
+        ).astype(BF16)
+        found.append(
+            lax.dot_general(
+                table, matrix, (((1,), (1,)), ((), ())), preferred_element_type=F32
+            )
+        )
+    low = iota((TILES // 2, LANES), 1) < GROUP
+    result = []
+    for at in range(len(labels)):
+        even = jnp.concatenate([f[at : at + 1, :] for f in found[0::2]], axis=0)
+        odd = jnp.concatenate([f[at : at + 1, :] for f in found[1::2]], axis=0)
+        rows = []
+        for j in range(TILES // 2):
+            lanes = slice(j * LANES, (j + 1) * LANES)
+            rows.append(jnp.where(low, even[:, lanes], pltpu.roll(odd[:, lanes], GROUP, 1)))
+            rows.append(jnp.where(low, pltpu.roll(even[:, lanes], GROUP, 1), odd[:, lanes]))
+        result.append(rows)
+    return result
+
+
+def one_level(row, base, weight=None):
+    wanted = iota((WIDE, row.shape[1]), 0).astype(F32).astype(BF16)
+    hit = wanted == (row - base).astype(BF16)
+    if weight is None:
+        weight = jnp.ones((1, row.shape[1]), BF16)
+    return jnp.where(hit, weight, jnp.zeros((1, row.shape[1]), BF16))
+
+
+def second_level(places, weights=None):
+    parts = []
+    for q in range(TILES // 2):
+        weight = None if weights is None else weights[q : q + 1, :].astype(BF16)
+        parts.append(one_level(places[q : q + 1, :], 1.0, weight))
+    return jnp.concatenate(parts, axis=1)
+
+
+def fill_message_two(msg_ref, row, local, m_ref, v_ref, held_ref):
+    def chunk_codes(k):
+        here = pl.ds(k * WIDE, WIDE)
+        return jnp.concatenate([m_ref[here, :], v_ref[here, :]], axis=1)
+
+    (places,) = sort_chunks(row, (local + 1.0,), chunk_codes, held_ref)
+    for t in range(TILES):
+        rows = times(second_level(places[t]), held_ref[t]).astype(BF16)
+        for p in range(WIDE // PAIR):
+            for j in range(2 * HALVES):
+                at = (t * WIDE // PAIR + p) * STRIDE + j * PAIR
+                msg_ref[at : at + PAIR, :] = rows[
+                    p * PAIR : (p + 1) * PAIR, j * LANES : (j + 1) * LANES
+                ]
+
+
 def fill_message(msg_ref, slot_rows, m_codes, v_codes, tile=512, step=256):
     for t in range(SAVED // tile):
         matrix = jnp.concatenate(
@@ -97,7 +191,7 @@
 
 
 def prepare(target_hbm, ms_hbm, vs_hbm, grad_hbm, m_hbm, v_hbm, msg_ref, *scratch):
-    refs, sem = scratch[:-1], scratch[-1]
+    refs, held_ref, sem = scratch[:-2], scratch[-2], scratch[-1]
     copies = [
         pltpu.make_async_copy(source, ref, sem.at[k])
         for k, (source, ref) in enumerate(
@@ -122,32 +216,34 @@
         ms_ref[...].astype(F32),
         vs_ref[...].astype(F32),
     )
-    before = one_hot(iota((LANES, 2 * LANES), 0) < iota((LANES, 2 * LANES), 1))
-    peer = iota((PEERS, LANES), 0).astype(F32)
-    nth = iota((PAIR, LANES), 0).astype(F32)
+    lanes = (WIDE, WIDE + LANES)
+    before = one_hot((iota(lanes, 0) < iota(lanes, 1)) | (iota(lanes, 1) >= WIDE))
+    dest, values = paired_rows(dest), [paired_rows(v) for v in values]
+    peer = iota((PEERS, WIDE), 0).astype(F32)
+    nth = iota((PAIR, WIDE), 0).astype(F32)
     carry = jnp.zeros((PEERS, LANES), F32)
     side = jnp.zeros((PEERS, LANES), F32)
-    slot_rows = []
+    slots = []
     total = jnp.zeros((8, grad_ref.shape[1]), F32)
-    for k in range(CHUNKS):
-        if k == CHUNKS // 2:
+    for k in range(TILES):
+        if k == TILES // 2:
             copies[3].wait()
-        if k >= CHUNKS // 2:
-            share = 2 * ROWS // CHUNKS
-            g = grad_ref[(k - CHUNKS // 2) * share : (k - CHUNKS // 2 + 1) * share, :].astype(F32)
+        if k >= TILES // 2:
+            share = 2 * ROWS // TILES
+            g = grad_ref[(k - TILES // 2) * share : (k - TILES // 2 + 1) * share, :].astype(F32)
             total = total + jnp.sum((g * g).reshape(-1, 8, g.shape[1]), axis=0)
         dest_row = dest[k : k + 1, :]
         hit = peer == dest_row
         hot = one_hot(hit)
         counts = times(hot, before)
-        ahead = counts[:, :LANES] + carry
-        carry = carry + counts[:, LANES:]
+        ahead = counts[:, :WIDE] + jnp.concatenate([carry, carry], axis=1)
+        carry = carry + counts[:, WIDE:]
         rank = jnp.sum(jnp.where(hit, ahead, 0.0), axis=0, keepdims=True)
-        slot_rows.append(dest_row * PAIR + rank)
+        slots.append(dest_row * PAIR + rank)
         ranked = nth == rank
         table = jnp.concatenate(
             [jnp.where(ranked, v[k : k + 1, :], 0.0) for v in values]
-            + [jnp.zeros((LANES - 4 * PAIR, LANES), F32)],
+            + [jnp.zeros((LANES - 4 * PAIR, WIDE), F32)],
             axis=0,
         ).astype(BF16)
         side = side + lax.dot_general(
@@ -170,7 +266,18 @@
         msg_ref[at : at + SIDE, :] = side[p * SIDE : (p + 1) * SIDE, :]
     for copy in copies[4:]:
         copy.wait()
-    fill_message(msg_ref, slot_rows, m_ref[...], v_ref[...])
+    local, row, fits = grouped(jnp.concatenate(slots, axis=0))
+
+    @pl.when(fits)
+    def _():
+        fill_message_two(msg_ref, row, local, m_ref, v_ref, held_ref)
+
+    @pl.when(jnp.logical_not(fits))
+    def _():
+        slot_rows = [
+            slot[:, lanes] for slot in slots for lanes in (slice(0, LANES), slice(LANES, WIDE))
+        ]
+        fill_message(msg_ref, slot_rows, m_ref[...], v_ref[...])
 
 
 def received(msg_ref, part):
@@ -227,74 +334,105 @@
     return rows[0] if len(rows) == 1 else jnp.concatenate(rows, axis=1)
 
 
-def scattered(place_rows, scale_rows, first, count, codes):
-    matrix = jnp.concatenate(
+def received_chunk(msg_ref, k):
+    first = k * (WIDE // PAIR) * STRIDE
+    return jnp.concatenate(
         [
-            picked_rows(place_rows, float(c * ROWS + first), count, scale_rows)
-            for c in range(COLB)
+            jnp.concatenate(
+                [
+                    msg_ref[at : at + PAIR, :]
+                    for at in range(
+                        first + j * PAIR, first + j * PAIR + (WIDE // PAIR) * STRIDE, STRIDE
+                    )
+                ],
+                axis=0,
+            )
+            for j in range(2 * HALVES)
         ],
-        axis=0,
-    )
-    return times(matrix, codes)
+        axis=1,
+    )
 
 
 def update(msg_ref, grad_ref, param_ref, *rest):
-    outs, held, sem = rest[:5], rest[5:10], rest[10]
+    outs, held, held_ref, sem = rest[:5], rest[5:10], rest[10], rest[11]
     new_ref, m_ref, ml_ref, v_ref, vl_ref = held
     place, m_scales, v_scales, factor = decode_side(msg_ref)
     place_rows = [place[k : k + 1, :] for k in range(CHUNKS)]
-    m_rows = [m_scales[k : k + 1, :].astype(BF16) for k in range(CHUNKS)]
-    v_rows = [v_scales[k : k + 1, :].astype(BF16) for k in range(CHUNKS)]
-    m_codes, v_codes = received(msg_ref, 0), received(msg_ref, 1)
-    gain = factor * (1.0 - beta_one)
-
-    def previous(first):
-        return (
-            scattered(place_rows, m_rows, first, TILE, m_codes),
-            scattered(place_rows, v_rows, first, TILE, v_codes),
-        )
-
-    def finish_tile(first, m_prev, v_prev):
-        here = pl.ds(first, TILE)
-        for c in range(COLB):
-            columns = pl.ds(c * BLOCK, BLOCK)
-            part = slice(c * TILE, (c + 1) * TILE)
-            added = grad_ref[here, columns].astype(F32) * gain
-            m_next = beta_one * m_prev[part, :] + added
-            largest = jnp.max(jnp.abs(m_next), axis=1, keepdims=True)
-            m_ref[here, columns] = (m_next * (1.0 / (largest + guard))).astype(BF16)
-            ml_ref[c : c + 1, here] = as_row(largest, TILE)
-            v_next = beta_two * v_prev[part, :] + added * added * (
-                (1.0 - beta_two) / (1.0 - beta_one) ** 2
+    m_rows = [m_scales[k : k + 1, :] for k in range(CHUNKS)]
+    v_rows = [v_scales[k : k + 1, :] for k in range(CHUNKS)]
+    m_gain = factor * ((1.0 - beta_one) / beta_one)
+    v_gain = factor * math.sqrt((1.0 - beta_two) / beta_two)
+    local, row, fits = grouped(paired(place_rows))
+
+    def finish_tile(t, m_prev, v_prev):
+        here = pl.ds((t % HALF) * WIDE, WIDE)
+        c = t // HALF
+        columns = pl.ds(c * BLOCK, BLOCK)
+        g = grad_ref[here, columns].astype(F32)
+        m_part = m_prev + g * m_gain
+        largest = jnp.max(jnp.abs(m_part), axis=1, keepdims=True)
+        m_ref[here, columns] = (m_part * (1.0 / (largest + guard / beta_one))).astype(BF16)
+        ml_ref[c : c + 1, here] = as_row(largest, WIDE) * beta_one
+        v_root = g * v_gain
+        v_part = v_prev + v_root * v_root
+        largest = jnp.max(v_part, axis=1, keepdims=True)
+        v_ref[here, columns] = (v_part * (1.0 / (largest + guard / beta_two))).astype(BF16)
+        vl_ref[c : c + 1, here] = as_row(largest, WIDE) * beta_two
+        root = v_part * lax.rsqrt(v_part) * V_UNIT + adam_eps / M_UNIT
+        new_ref[here, columns] = (param_ref[here, columns].astype(F32) - m_part / root).astype(BF16)
+
+    def run(previous):
+        copies = []
+
+        def send(k, here):
+            copies.append(
+                pltpu.make_async_copy(held[k].at[here], outs[k].at[here], sem.at[len(copies)])
             )
-            largest = jnp.max(v_next, axis=1, keepdims=True)
-            v_ref[here, columns] = (v_next * (1.0 / (largest + guard))).astype(BF16)
-            vl_ref[c : c + 1, here] = as_row(largest, TILE)
-            square = v_next * (1.0 / (1.0 - beta_two**step_count))
-            root = square * lax.rsqrt(square)
-            step = m_next * (learn_rate / (1.0 - beta_one**step_count)) / (root + adam_eps)
-            new_ref[here, columns] = (param_ref[here, columns].astype(F32) - step).astype(BF16)
-
-    copies = []
-
-    def send(k, here):
-        copies.append(
-            pltpu.make_async_copy(held[k].at[here], outs[k].at[here], sem.at[len(copies)])
-        )
-        copies[-1].start()
-
-    ahead = previous(0)
-    for first in range(0, ROWS, TILE):
-        now = ahead
-        if first + TILE < ROWS:
-            ahead = previous(first + TILE)
-        finish_tile(first, *now)
-        for k in (0, 1, 3):
-            send(k, pl.ds(first, TILE))
-    for k in (2, 4):
-        send(k, pl.ds(0, COLB))
-    for copy in copies:
-        copy.wait()
+            copies[-1].start()
+
+        order = [c * HALF + h for h in range(HALF) for c in range(COLB)]
+        ahead = previous(order[0])
+        for at, t in enumerate(order):
+            now = ahead
+            if at + 1 < len(order):
+                ahead = previous(order[at + 1])
+            finish_tile(t, *now)
+            for k in (0, 1, 3):
+                send(k, (pl.ds((t % HALF) * WIDE, WIDE), pl.ds(t // HALF * BLOCK, BLOCK)))
+        for k in (2, 4):
+            send(k, pl.ds(0, COLB))
+        for copy in copies:
+            copy.wait()
+
+    @pl.when(fits)
+    def _():
+        labels = (local + 1.0, paired(m_rows), paired(v_rows))
+        places, m_weights, v_weights = sort_chunks(
+            row, labels, functools.partial(received_chunk, msg_ref), held_ref
+        )
+
+        def previous(t):
+            return (
+                times(second_level(places[t], m_weights[t]), held_ref[t, :, :BLOCK]),
+                times(second_level(places[t], v_weights[t]), held_ref[t, :, BLOCK:]),
+            )
+
+        run(previous)
+
+    @pl.when(jnp.logical_not(fits))
+    def _():
+        def previous(t):
+            return tuple(
+                times(
+                    picked_rows(
+                        place_rows, float(t * WIDE), WIDE, [w.astype(BF16) for w in weights]
+                    ),
+                    received(msg_ref, part),
+                )
+                for part, weights in enumerate((m_rows, v_rows))
+            )
+
+        run(previous)
 
 
 def shaped(shape, dtype):
@@ -305,7 +443,7 @@
     return pl.BlockSpec(shape, lambda i: (0,) * len(shape))
 
 
-TILE = 128
+HALF = ROWS // WIDE
 
 
 def make_message(grad2, m_codes, v_codes, m_scales, v_scales, block_target):
@@ -322,6 +460,7 @@
         in_specs=[pl.BlockSpec(memory_space=pltpu.HBM)] * len(arrays),
         out_shape=pltpu.VMEM((PEERS * STRIDE, LANES), BF16),
         scratch_shapes=[pltpu.VMEM(a.shape, a.dtype) for a in arrays]
+        + [pltpu.VMEM((TILES, TILES * GROUP, 2 * BLOCK), BF16)]
         + [pltpu.SemaphoreType.DMA((len(arrays),))],
         name="prepare",
         compiler_params=pltpu.CompilerParams(vmem_limit_bytes=VMEM_LIMIT),
@@ -338,7 +477,10 @@
         out_specs=[pl.BlockSpec(memory_space=pltpu.HBM)] * len(outs),
         out_shape=tuple(pltpu.HBM(*o) for o in outs),
         scratch_shapes=[pltpu.VMEM(*o) for o in outs]
-        + [pltpu.SemaphoreType.DMA((3 * ROWS // TILE + 2,))],
+        + [
+            pltpu.VMEM((TILES, TILES * GROUP, 2 * BLOCK), BF16),
+            pltpu.SemaphoreType.DMA((3 * TILES + 2,)),
+        ],
         name="update",
         compiler_params=pltpu.CompilerParams(vmem_limit_bytes=VMEM_LIMIT),
     )(*(pltpu.with_memory_space_constraint(a, pltpu.VMEM) for a in (got, grad2, param2)))

time: 54.4 us -> 52.6 us (0.967)
  Pallas kernels: 13.1 us -> 11.1 us
    pallas_call x1, Pallas kernels: 6.67 us -> 5.4 us  [make_message(): pl.pallas_call(prepare, in_specs=[pl.BlockSpec(memory_space=pltpu.HBM)] *...]
    pallas_call x1, Pallas kernels: 6.42 us -> 5.75 us  [finish(): pl.pallas_call(update, in_specs=[pl.BlockSpec(memory_space=pltpu.VMEM)] *...]
where the time goes in v4:
time: 52.6 us; the launch traced here: 52.5 us
  blocking collectives  40.5 us (77%)
  Pallas kernels  11.1 us (21%)
  between operations  0.82 us (2%)
    all_to_all x1, blocking collectives, body(): lax.all_to_all(pairs, EXCHANGE, split_axis=0, concat_axis=0, tiled=True)  40.5 us
    pallas_call x1, Pallas kernels, finish(): pl.pallas_call(update, in_specs=[pl.BlockSpec(memory_space=pltpu.VMEM)] *...  5.75 us
    pallas_call x1, Pallas kernels, make_message(): pl.pallas_call(prepare, in_specs=[pl.BlockSpec(memory_space=pltpu.HBM)] *...  5.4 us

profile of v4, /device:TPU:1, one launch (start us, length us, event | category | flops | bytes accessed | tf_op | source)
XLA Modules:
  0.0 52.5 jit_solution(3154178715814359678)
XLA Ops:
  0.6 5.4 %prepare.1 = bf16[8448,128]{1,0:T(8,128)(2,1)S(1)} custom-call(s32[16,128]{1,0:T(8,128)} %bitcast.21, bf16[16,128]{1,0:T(8,128)(2,1)} %bitcast.22, bf16[16,128]{1,0:T(8,128)(2,1)} %bitcast.23, bf16[512,1024]{1,0:T(8,128)(2,1)} %bitcast.18, bf16[2048,256]{1,0:T(8,128)(2,1)} %m_hbm.1, bf16[2048,256]{1,0:T(8,128)(2,1)} %v_hbm.1), custom_call_target="tpu_custom_call" | custom-call | tf_op jit(solution)/shard_map/prepare/pallas_call | solution.py:458
  6.0 0.0 copy-start
  6.1 0.0 copy-start.1
  6.1 40.5 %all_to_all.5 = bf16[128,33,2,128]{3,2,1,0:T(2,128)(2,1)S(1)} all-to-all(bf16[128,33,2,128]{3,2,1,0:T(2,128)(2,1)S(1)} %bitcast.17), channel_id=1, replica_groups=mesh['fsdp_0'=4,'fsdp_1'=2,'fsdp_2'=2,'tp_0'=4,'tp_1'=2] {'fsdp_2','fsdp..., dimensions={0} | all-to-all | bytes 4325376 | tf_op jit(solution)/shard_map/all_to_all | solution.py:494
  46.5 0.0 copy-done
  46.5 0.0 copy-done.1
  46.5 5.7 %update.1 = (bf16[512,1024]{1,0:T(8,128)(2,1)}, bf16[512,1024]{1,0:T(8,128)(2,1)}, f32[4,512]{1,0:T(4,128)}, bf16[512,1024]{1,0:T(8,128)(2,1)}, f32[4,512]{1,0:T(4,128)}) custom-call(bf16[8448,128]{1,0:T(8,128)(2,1)S(1)} %bitcast.16, bf16[512,1024]{1,0:T(8,128)(2,1)S(1)} %bitcast.19, bf16[512,1024]{1,0:T(8,128)(2,1)S(1)} %bitcast.20), custom_call_target="tpu_custom_call" | custom-call | tf_op jit(solution)/shard_map/update/pallas_call | solution.py:474
Async XLA Ops:
  6.0 40.5 %copy-start = (bf16[1,512,1024]{2,1,0:T(8,128)(2,1)S(1)}, bf16[1,512,1024]{2,1,0:T(8,128)(2,1)}, u32[]{:S(2)}) copy-start(bf16[1,512,1024]{2,1,0:T(8,128)(2,1)} %param.8) | copy-start | bytes 3145732
  6.1 40.5 %copy-start.1 = (bf16[1,512,1024]{2,1,0:T(8,128)(2,1)S(1)}, bf16[1,512,1024]{2,1,0:T(8,128)(2,1)}, u32[]{:S(2)}) copy-start(bf16[1,512,1024]{2,1,0:T(8,128)(2,1)} %param.7) | copy-start | bytes 3145732

commit v5 on v4

--- a/solution.py
+++ b/solution.py
@@ -106,7 +106,7 @@
     return target - tile * WIDE, tile * GROUP + rank, fits
 
 
-def sort_chunks(row, labels, chunk_codes, held_ref):
+def sort_chunks(row, labels, chunk_codes, held_ref, label_ref):
     found = []
     for k in range(TILES):
         step = SAVED // TILES
@@ -125,17 +125,17 @@
             )
         )
     low = iota((TILES // 2, LANES), 1) < GROUP
-    result = []
     for at in range(len(labels)):
         even = jnp.concatenate([f[at : at + 1, :] for f in found[0::2]], axis=0)
         odd = jnp.concatenate([f[at : at + 1, :] for f in found[1::2]], axis=0)
-        rows = []
         for j in range(TILES // 2):
             lanes = slice(j * LANES, (j + 1) * LANES)
-            rows.append(jnp.where(low, even[:, lanes], pltpu.roll(odd[:, lanes], GROUP, 1)))
-            rows.append(jnp.where(low, pltpu.roll(even[:, lanes], GROUP, 1), odd[:, lanes]))
-        result.append(rows)
-    return result
+            label_ref[at, 2 * j] = jnp.where(
+                low, even[:, lanes], pltpu.roll(odd[:, lanes], GROUP, 1)
+            )
+            label_ref[at, 2 * j + 1] = jnp.where(
+                low, pltpu.roll(even[:, lanes], GROUP, 1), odd[:, lanes]
+            )
 
 
 def one_level(row, base, weight=None):
@@ -154,14 +154,9 @@
     return jnp.concatenate(parts, axis=1)
 
 
-def fill_message_two(msg_ref, row, local, m_ref, v_ref, held_ref):
-    def chunk_codes(k):
-        here = pl.ds(k * WIDE, WIDE)
-        return jnp.concatenate([m_ref[here, :], v_ref[here, :]], axis=1)
-
-    (places,) = sort_chunks(row, (local + 1.0,), chunk_codes, held_ref)
+def fill_message_two(msg_ref, held_ref, label_ref):
     for t in range(TILES):
-        rows = times(second_level(places[t]), held_ref[t]).astype(BF16)
+        rows = times(second_level(label_ref[0, t]), held_ref[t]).astype(BF16)
         for p in range(WIDE // PAIR):
             for j in range(2 * HALVES):
                 at = (t * WIDE // PAIR + p) * STRIDE + j * PAIR
@@ -191,7 +186,7 @@
 
 
 def prepare(target_hbm, ms_hbm, vs_hbm, grad_hbm, m_hbm, v_hbm, msg_ref, *scratch):
-    refs, held_ref, sem = scratch[:-2], scratch[-2], scratch[-1]
+    refs, (held_ref, label_ref, sem) = scratch[:-3], scratch[-3:]
     copies = [
         pltpu.make_async_copy(source, ref, sem.at[k])
         for k, (source, ref) in enumerate(
@@ -201,6 +196,8 @@
     for copy in copies:
         copy.start()
     target_ref, ms_ref, vs_ref, grad_ref, m_ref, v_ref = refs
+    lanes = (WIDE, WIDE + LANES)
+    before = one_hot((iota(lanes, 0) < iota(lanes, 1)) | (iota(lanes, 1) >= WIDE))
     for copy in copies[:3]:
         copy.wait()
     target = target_ref[...]
@@ -216,22 +213,13 @@
         ms_ref[...].astype(F32),
         vs_ref[...].astype(F32),
     )
-    lanes = (WIDE, WIDE + LANES)
-    before = one_hot((iota(lanes, 0) < iota(lanes, 1)) | (iota(lanes, 1) >= WIDE))
     dest, values = paired_rows(dest), [paired_rows(v) for v in values]
     peer = iota((PEERS, WIDE), 0).astype(F32)
     nth = iota((PAIR, WIDE), 0).astype(F32)
     carry = jnp.zeros((PEERS, LANES), F32)
     side = jnp.zeros((PEERS, LANES), F32)
     slots = []
-    total = jnp.zeros((8, grad_ref.shape[1]), F32)
     for k in range(TILES):
-        if k == TILES // 2:
-            copies[3].wait()
-        if k >= TILES // 2:
-            share = 2 * ROWS // TILES
-            g = grad_ref[(k - TILES // 2) * share : (k - TILES // 2 + 1) * share, :].astype(F32)
-            total = total + jnp.sum((g * g).reshape(-1, 8, g.shape[1]), axis=0)
         dest_row = dest[k : k + 1, :]
         hit = peer == dest_row
         hot = one_hot(hit)
@@ -249,31 +237,53 @@
         side = side + lax.dot_general(
             hot, table, (((1,), (1,)), ((), ())), preferred_element_type=F32
         )
-    total = jnp.sum(jnp.sum(total, axis=1, keepdims=True), axis=0, keepdims=True)
-    high = total.astype(BF16).astype(F32)
-    middle = (total - high).astype(BF16).astype(F32)
-    low = total - high - middle
-    lane = iota((PEERS, LANES), 1)
-    side = jnp.where(lane == 64, high, side)
-    side = jnp.where(lane == 65, middle, side)
-    side = jnp.where(lane == 66, low, side).astype(BF16)
-    spread = one_hot(
-        lax.shift_right_logical(iota((PEERS * SIDE, PEERS), 0), 1) == iota((PEERS * SIDE, PEERS), 1)
-    )
-    side = times(spread, side).astype(BF16)
-    for p in range(PEERS):
-        at = p * STRIDE + MSG_ROWS
-        msg_ref[at : at + SIDE, :] = side[p * SIDE : (p + 1) * SIDE, :]
-    for copy in copies[4:]:
+    local, row, fits = grouped(jnp.concatenate(slots, axis=0))
+    for copy in copies[3:]:
         copy.wait()
-    local, row, fits = grouped(jnp.concatenate(slots, axis=0))
+
+    def squares(k):
+        share = ROWS // TILES
+        g = grad_ref[k * share : (k + 1) * share, :].astype(F32)
+        return jnp.sum((g * g).reshape(-1, 8, g.shape[1]), axis=0)
+
+    def fill_side(total):
+        total = jnp.sum(jnp.sum(total, axis=1, keepdims=True), axis=0, keepdims=True)
+        high = total.astype(BF16).astype(F32)
+        middle = (total - high).astype(BF16).astype(F32)
+        low = total - high - middle
+        lane = iota((PEERS, LANES), 1)
+        whole_side = jnp.where(lane == 64, high, side)
+        whole_side = jnp.where(lane == 65, middle, whole_side)
+        whole_side = jnp.where(lane == 66, low, whole_side).astype(BF16)
+        spread = one_hot(
+            lax.shift_right_logical(iota((PEERS * SIDE, PEERS), 0), 1)
+            == iota((PEERS * SIDE, PEERS), 1)
+        )
+        doubled = times(spread, whole_side).astype(BF16)
+        for p in range(PEERS):
+            at = p * STRIDE + MSG_ROWS
+            msg_ref[at : at + SIDE, :] = doubled[p * SIDE : (p + 1) * SIDE, :]
 
     @pl.when(fits)
     def _():
-        fill_message_two(msg_ref, row, local, m_ref, v_ref, held_ref)
+        sums = []
+
+        def chunk_codes(k):
+            sums.append(squares(k))
+            here = pl.ds(k * WIDE, WIDE)
+            return jnp.concatenate([m_ref[here, :], v_ref[here, :]], axis=1)
+
+        sort_chunks(row, (local + 1.0,), chunk_codes, held_ref, label_ref)
+        fill_side(sum(sums[1:], sums[0]))
+
+    @pl.when(fits)
+    def _():
+        fill_message_two(msg_ref, held_ref, label_ref)
 
     @pl.when(jnp.logical_not(fits))
     def _():
+        sums = [squares(k) for k in range(TILES)]
+        fill_side(sum(sums[1:], sums[0]))
         slot_rows = [
             slot[:, lanes] for slot in slots for lanes in (slice(0, LANES), slice(LANES, WIDE))
         ]
@@ -298,25 +308,25 @@
 
 def decode_side(msg_ref):
     raw = jnp.concatenate(
-        [
-            msg_ref[at : at + PAIR, :]
-            for at in range(STRIDE - PAIR, PEERS * STRIDE, STRIDE)
-        ],
-        axis=0,
-    )
-    gather = one_hot(
-        iota((PEERS, PEERS * PAIR), 1) == iota((PEERS, PEERS * PAIR), 0) * PAIR + (PAIR - SIDE)
-    )
+        [msg_ref[at : at + SIDE, :] for at in range(MSG_ROWS, PEERS * STRIDE, STRIDE)], axis=0
+    )
+    gather = one_hot(iota((PEERS, PEERS * SIDE), 1) == iota((PEERS, PEERS * SIDE), 0) * SIDE)
     side = times(gather, raw)
     lane = iota((PEERS, LANES), 1)
     own = lax.shift_right_logical(lane, 4) == (iota((PEERS, LANES), 0) & 7)
-    rows = []
-    for q in range(4):
-        widen = one_hot(
-            iota((LANES, LANES), 0) == q * PAIR + (iota((LANES, LANES), 1) & (PAIR - 1))
-        )
-        wide = times(side.astype(BF16), widen)
-        rows.append(jnp.sum(jnp.where(own, wide, 0.0).reshape(CHUNKS, 8, LANES), axis=1))
+    field = (LANES, 4 * LANES)
+    widen = one_hot(
+        iota(field, 0)
+        == lax.shift_right_logical(iota(field, 1), 7) * PAIR + (iota(field, 1) & (PAIR - 1))
+    )
+    wide = times(side.astype(BF16), widen)
+    rows = [
+        jnp.sum(
+            jnp.where(own, wide[:, q * LANES : (q + 1) * LANES], 0.0).reshape(CHUNKS, 8, LANES),
+            axis=1,
+        )
+        for q in range(4)
+    ]
     sums = jnp.where((lane >= 64) & (lane < 67), side, 0.0)
     square_sum = jnp.sum(jnp.sum(sums, axis=1, keepdims=True), axis=0, keepdims=True)
     root_mean = jnp.sqrt(square_sum / (LAYERS * D * D) + guard)
@@ -354,7 +364,7 @@
 
 
 def update(msg_ref, grad_ref, param_ref, *rest):
-    outs, held, held_ref, sem = rest[:5], rest[5:10], rest[10], rest[11]
+    outs, held, held_ref, label_ref, gm_ref, gv_ref, sem = rest[:5], rest[5:10], *rest[10:]
     new_ref, m_ref, ml_ref, v_ref, vl_ref = held
     place, m_scales, v_scales, factor = decode_side(msg_ref)
     place_rows = [place[k : k + 1, :] for k in range(CHUNKS)]
@@ -364,17 +374,22 @@
     v_gain = factor * math.sqrt((1.0 - beta_two) / beta_two)
     local, row, fits = grouped(paired(place_rows))
 
+    def gradient_terms(k):
+        here = pl.ds(k * (ROWS // TILES), ROWS // TILES)
+        g = grad_ref[here, :].astype(F32)
+        v_root = g * v_gain
+        gm_ref[here, :] = g * m_gain
+        gv_ref[here, :] = v_root * v_root
+
     def finish_tile(t, m_prev, v_prev):
         here = pl.ds((t % HALF) * WIDE, WIDE)
         c = t // HALF
         columns = pl.ds(c * BLOCK, BLOCK)
-        g = grad_ref[here, columns].astype(F32)
-        m_part = m_prev + g * m_gain
+        m_part = m_prev + gm_ref[here, columns]
         largest = jnp.max(jnp.abs(m_part), axis=1, keepdims=True)
         m_ref[here, columns] = (m_part * (1.0 / (largest + guard / beta_one))).astype(BF16)
         ml_ref[c : c + 1, here] = as_row(largest, WIDE) * beta_one
-        v_root = g * v_gain
-        v_part = v_prev + v_root * v_root
+        v_part = v_prev + gv_ref[here, columns]
         largest = jnp.max(v_part, axis=1, keepdims=True)
         v_ref[here, columns] = (v_part * (1.0 / (largest + guard / beta_two))).astype(BF16)
         vl_ref[c : c + 1, here] = as_row(largest, WIDE) * beta_two
@@ -407,20 +422,29 @@
     @pl.when(fits)
     def _():
         labels = (local + 1.0, paired(m_rows), paired(v_rows))
-        places, m_weights, v_weights = sort_chunks(
-            row, labels, functools.partial(received_chunk, msg_ref), held_ref
-        )
-
+
+        def chunk_codes(k):
+            gradient_terms(k)
+            return received_chunk(msg_ref, k)
+
+        sort_chunks(row, labels, chunk_codes, held_ref, label_ref)
+
+    @pl.when(fits)
+    def _():
         def previous(t):
+            places = label_ref[0, t]
             return (
-                times(second_level(places[t], m_weights[t]), held_ref[t, :, :BLOCK]),
-                times(second_level(places[t], v_weights[t]), held_ref[t, :, BLOCK:]),
+                times(second_level(places, label_ref[1, t]), held_ref[t, :, :BLOCK]),
+                times(second_level(places, label_ref[2, t]), held_ref[t, :, BLOCK:]),
             )
 
         run(previous)
 
     @pl.when(jnp.logical_not(fits))
     def _():
+        for k in range(TILES):
+            gradient_terms(k)
+
         def previous(t):
             return tuple(
                 times(
@@ -461,6 +485,7 @@
         out_shape=pltpu.VMEM((PEERS * STRIDE, LANES), BF16),
         scratch_shapes=[pltpu.VMEM(a.shape, a.dtype) for a in arrays]
         + [pltpu.VMEM((TILES, TILES * GROUP, 2 * BLOCK), BF16)]
+        + [pltpu.VMEM((1, TILES, TILES // 2, LANES), F32)]
         + [pltpu.SemaphoreType.DMA((len(arrays),))],
         name="prepare",
         compiler_params=pltpu.CompilerParams(vmem_limit_bytes=VMEM_LIMIT),
@@ -479,6 +504,9 @@
         scratch_shapes=[pltpu.VMEM(*o) for o in outs]
         + [
             pltpu.VMEM((TILES, TILES * GROUP, 2 * BLOCK), BF16),
+            pltpu.VMEM((3, TILES, TILES // 2, LANES), F32),
+            pltpu.VMEM((ROWS, COLB * BLOCK), F32),
+            pltpu.VMEM((ROWS, COLB * BLOCK), F32),
             pltpu.SemaphoreType.DMA((3 * TILES + 2,)),
         ],
         name="update",

time: 52.6 us -> 52.1 us (level)
  no operation moved by 1% of the time
where the time goes in v5:
time: 52.1 us; the launch traced here: 51.9 us
  blocking collectives  40.5 us (78%)
  Pallas kernels  10.6 us (20%)
  between operations  0.82 us (2%)
    all_to_all x1, blocking collectives, body(): lax.all_to_all(pairs, EXCHANGE, split_axis=0, concat_axis=0, tiled=True)  40.5 us
    pallas_call x1, Pallas kernels, finish(): pl.pallas_call(update, in_specs=[pl.BlockSpec(memory_space=pltpu.VMEM)] *...  5.62 us
    pallas_call x1, Pallas kernels, make_message(): pl.pallas_call(prepare, in_specs=[pl.BlockSpec(memory_space=pltpu.HBM)] *...  5 us

profile of v5, /device:TPU:1, one launch (start us, length us, event | category | flops | bytes accessed | tf_op | source)
XLA Modules:
  0.0 51.9 jit_solution(13837098917525871841)
XLA Ops:
  0.6 5.0 %prepare.1 = bf16[8448,128]{1,0:T(8,128)(2,1)S(1)} custom-call(s32[16,128]{1,0:T(8,128)} %bitcast.21, bf16[16,128]{1,0:T(8,128)(2,1)} %bitcast.22, bf16[16,128]{1,0:T(8,128)(2,1)} %bitcast.23, bf16[512,1024]{1,0:T(8,128)(2,1)} %bitcast.18, bf16[2048,256]{1,0:T(8,128)(2,1)} %m_hbm.1, bf16[2048,256]{1,0:T(8,128)(2,1)} %v_hbm.1), custom_call_target="tpu_custom_call" | custom-call | tf_op jit(solution)/shard_map/prepare/pallas_call | solution.py:482
  5.6 0.0 copy-start
  5.7 0.0 copy-start.1
  5.7 40.5 %all_to_all.5 = bf16[128,33,2,128]{3,2,1,0:T(2,128)(2,1)S(1)} all-to-all(bf16[128,33,2,128]{3,2,1,0:T(2,128)(2,1)S(1)} %bitcast.17), channel_id=1, replica_groups=mesh['fsdp_0'=4,'fsdp_1'=2,'fsdp_2'=2,'tp_0'=4,'tp_1'=2] {'fsdp_2','fsdp..., dimensions={0} | all-to-all | bytes 4325376 | tf_op jit(solution)/shard_map/all_to_all | solution.py:522
  46.1 0.0 copy-done
  46.1 0.0 copy-done.1
  46.1 5.6 %update.1 = (bf16[512,1024]{1,0:T(8,128)(2,1)}, bf16[512,1024]{1,0:T(8,128)(2,1)}, f32[4,512]{1,0:T(4,128)}, bf16[512,1024]{1,0:T(8,128)(2,1)}, f32[4,512]{1,0:T(4,128)}) custom-call(bf16[8448,128]{1,0:T(8,128)(2,1)S(1)} %bitcast.16, bf16[512,1024]{1,0:T(8,128)(2,1)S(1)} %bitcast.19, bf16[512,1024]{1,0:T(8,128)(2,1)S(1)} %bitcast.20), custom_call_target="tpu_custom_call" | custom-call | tf_op jit(solution)/shard_map/update/pallas_call | solution.py:499
Async XLA Ops:
  5.6 40.5 %copy-start = (bf16[1,512,1024]{2,1,0:T(8,128)(2,1)S(1)}, bf16[1,512,1024]{2,1,0:T(8,128)(2,1)}, u32[]{:S(2)}) copy-start(bf16[1,512,1024]{2,1,0:T(8,128)(2,1)} %param.8) | copy-start | bytes 3145732
  5.7 40.5 %copy-start.1 = (bf16[1,512,1024]{2,1,0:T(8,128)(2,1)S(1)}, bf16[1,512,1024]{2,1,0:T(8,128)(2,1)}, u32[]{:S(2)}) copy-start(bf16[1,512,1024]{2,1,0:T(8,128)(2,1)} %param.7) | copy-start | bytes 3145732
